TPU v7x, 256 devices: a whole 4x4x8 slice. The times are simulated.
256 devices in a mesh: grp: 2 (over z_hi), gy: 4 (over z_lo), gz: 32 (over x, y, core).
Axes of the slice: x: 4, y: 4, z: 8 (z_hi: 2, z_lo: 4; z = z_hi * 4 + z_lo), core: 2. Of those that a mesh axis runs over, the one named last changes fastest.
Arguments:
- vorticity: float32 [2, 3, 256, 256, 256], P('grp', None, 'gz', 'gy'), may hold values from -6 to 6
- wind: float32 [2, 3], P('grp'), may hold values from 0.5 to 1.2
Outputs:
- new_vorticity: float32 [2, 3, 256, 256, 256], P('grp', None, 'gz', 'gy')
- velocity: float32 [2, 3, 256, 256, 256], P('grp', None, 'gz', 'gy')
All inputs are finite; a program needn't handle non-finite values.
Results may differ from a plain program's by a relative error of at most 0.0003.
Values sent between devices are 32-bit elements; how exact they have to be, the bound alone decides.
A program may use at most 128 MiB of HBM per device.

v0:
```python
import functools
import math

import jax
import jax.numpy as jnp
import numpy as np
from jax import lax
from jax.experimental import pallas as pl
from jax.experimental.pallas import tpu as pltpu
from jax.sharding import PartitionSpec as P

TIME_STEP = 0.4
MESH = pl.DeviceIdType.MESH
N = 256
HALF = 128
GY = 4
GZ = 32
PEERS = GY * GZ
LZ = 8
LY = 64


def split(values):
    high = values.astype(jnp.bfloat16)
    low = (values - high.astype(jnp.float32)).astype(jnp.bfloat16)
    return high, low


def table_pair(table):
    table = np.asarray(table, np.float32)
    high = table.astype(jnp.bfloat16)
    low = (table - high.astype(np.float32)).astype(jnp.bfloat16)
    return np.stack([high, low])


def make_tables():
    index = np.arange(N)
    angle = (index[:, None] * index[None, :] % N) * (2.0 * math.pi / N)
    cosine, sine = np.cos(angle), np.sin(angle)
    alternate = 1.0 - 2.0 * (index % 2)
    sine_in = -sine[:HALF].copy()
    sine_in[0] = alternate
    x_in = np.concatenate([cosine[:HALF], sine_in], 0)
    x_out = 2.0 * x_in / N
    x_out[0] *= 0.5
    x_out[HALF] *= 0.5
    cos_y = cosine.reshape(GY, 1, LY, N)
    sin_y = sine.reshape(GY, 1, LY, N)
    to_real = np.concatenate([cos_y, sin_y], 1).reshape(2 * N, N)
    to_imag = np.concatenate([-sin_y, cos_y], 1).reshape(2 * N, N)
    y_in = np.concatenate([to_real, to_imag], 1)
    y_out = np.concatenate([to_real, to_imag], 1).T / N
    z_all = np.stack([cosine, sine])
    return [table_pair(t) for t in (x_in, y_in, z_all, y_out, x_out)]


def dot3(a, b, dims=((1,), (0,))):
    def one(left, right):
        return lax.dot_general(left, right, (dims, ((), ())), preferred_element_type=jnp.float32)

    return one(a[0], b[0]) + (one(a[0], b[1]) + one(a[1], b[0]))


def each_peer(gy, gz, visit):
    for q in range(1, GY):
        visit(lax.rem(gy + q, GY), gz)

    def step(k, carry):
        other_z = lax.rem(gz + k, GZ)
        for q in range(GY):
            visit(lax.rem(gy + q, GY), other_z)
        return carry

    lax.fori_loop(1, GZ, step, 0)


def wait_bytes(ref, sem):
    pltpu.make_async_copy(ref, ref, sem).wait()


def waves(shape, axis):
    index = lax.broadcasted_iota(jnp.int32, shape, axis)
    signed = jnp.where(index < N // 2, index, index - N)
    full = signed.astype(jnp.float32) * (2.0 * math.pi / N)
    return full, jnp.where(index == N // 2, 0.0, full)


def spectral_kernel(
    field, wind, x_in, y_in, z_all, y_out, x_out, velocity,
    send, recv, stream, send2, recv2, scale, ssem, rsem, ssem2, rsem2,
):
    gy = lax.axis_index("gy")
    gz = lax.axis_index("gz")
    me = gy * GZ + gz
    barrier = pltpu.get_barrier_semaphore()

    def greet(other_y, other_z):
        pl.semaphore_signal(
            barrier, inc=1, device_id={"gy": other_y, "gz": other_z}, device_id_type=MESH
        )

    each_peer(gy, gz, greet)

    lane = lax.broadcasted_iota(jnp.int32, (HALF, 128), 1)
    first_half = lane < LY
    for c in (1, 2, 0):
        for b in range(2):
            rows = field[0, c, 4 * b : 4 * b + 4].reshape(4 * LY, N)
            lines = dot3((x_in[0], x_in[1]), split(rows), ((1,), (1,)))
            for t in range(2):
                real = lines[:HALF, 128 * t : 128 * t + 128]
                imag = lines[HALF:, 128 * t : 128 * t + 128]
                even = jnp.where(first_half, real, pltpu.roll(imag, LY, 1))
                odd = jnp.where(first_half, pltpu.roll(real, LY, 1), imag)
                z = 4 * b + 2 * t
                send[c, pl.ds(z, HALF, stride=LZ), :] = even
                send[c, pl.ds(z + 1, HALF, stride=LZ), :] = odd
    mine = pl.ds(pl.multiple_of(me * LZ, LZ), LZ)
    mine_z = pl.ds(pl.multiple_of(gz * LZ, LZ), LZ)
    pl.semaphore_wait(barrier, PEERS - 1)

    for c in (1, 2, 0):
        def out(other_y, other_z, c=c):
            other = other_y * GZ + other_z
            pltpu.make_async_remote_copy(
                send.at[c, pl.ds(pl.multiple_of(other * LZ, LZ), LZ)],
                recv.at[c, gy, mine_z],
                ssem.at[c],
                rsem.at[c],
                device_id={"gy": other_y, "gz": other_z},
                device_id_type=MESH,
            ).start()

        each_peer(gy, gz, out)
        recv[c, gy, mine_z, :] = send[c, mine, :]

    wave_z, curl_z = waves((N, N), 0)
    wave_y, curl_y = waves((N, N), 1)
    curl_x = me.astype(jnp.float32) * (2.0 * math.pi / N)
    squared = curl_x * curl_x + wave_y * wave_y + wave_z * wave_z
    positive = squared > 0
    scale[0] = jnp.where(positive, 1.0 / jnp.where(positive, squared, 1.0), 0.0)

    @pl.when(me == 0)
    def _():
        base = scale[0]
        top = 1.0 / (squared + math.pi * math.pi)
        scale[0] = 0.5 * (base + top)
        scale[1] = 0.5 * (base - top)

    curl = (curl_x, curl_y, curl_z)
    table_y = (y_in[0], y_in[1])
    cosine = (z_all[0, 0], z_all[1, 0])
    sine = (z_all[0, 1], z_all[1, 1])

    def transform(plane):
        lines = split(dot3(split(plane), table_y))
        by_cos = dot3(cosine, lines)
        by_sin = dot3(sine, lines)
        real = by_cos[:, :N] + by_sin[:, N:]
        imag = by_cos[:, N:] - by_sin[:, :N]
        return real, imag

    def forward(c):
        wait_bytes(recv2.at[c, pl.ds(0, (PEERS - 1) * LZ)], rsem.at[c])
        plane = jnp.concatenate([recv[c, j] for j in range(GY)], 1)
        real, imag = transform(plane)
        stream[c, 0] = real * scale[0]
        stream[c, 1] = imag * scale[0]

        @pl.when(me == 0)
        def _():
            column = lax.broadcasted_iota(jnp.int32, (N, 2 * N), 1)
            plane = jnp.concatenate([recv[c, j] for j in range(GY)], 1)
            real, imag = transform(jnp.where(column % 128 < LY, plane, -plane))
            stream[c, 0] += real * scale[1]
            stream[c, 1] += imag * scale[1]

    def backward(d):
        a, b = (d + 1) % 3, (d + 2) % 3
        real = curl[b] * stream[a, 1] - curl[a] * stream[b, 1]
        imag = curl[a] * stream[b, 0] - curl[b] * stream[a, 0]
        lines = split(jnp.concatenate([real, imag], 1))
        by_cos = dot3(cosine, lines)
        by_sin = dot3(sine, lines)
        real = by_cos[:, :N] - by_sin[:, N:]
        imag = by_cos[:, N:] + by_sin[:, :N]
        lines = split(jnp.concatenate([real, imag], 1) * (1.0 / N))
        plane = dot3(lines, (y_out[0], y_out[1]))
        for j in range(GY):
            send2[d, j] = plane[:, 128 * j : 128 * j + 128]

        def out(other_y, other_z):
            pltpu.make_async_remote_copy(
                send2.at[d, other_y, pl.ds(pl.multiple_of(other_z * LZ, LZ), LZ)],
                recv2.at[d, mine],
                ssem2.at[d],
                rsem2.at[d],
                device_id={"gy": other_y, "gz": other_z},
                device_id_type=MESH,
            ).start()

        each_peer(gy, gz, out)
        recv2[d, mine, :] = send2[d, gy, mine_z, :]

    forward(1)
    forward(2)
    backward(0)
    forward(0)
    backward(1)
    backward(2)

    for d in range(3):
        wait_bytes(recv2.at[d, pl.ds(0, (PEERS - 1) * LZ)], rsem2.at[d])
        drift = wind[0, d]
        for b in range(2):
            parts = []
            for z in range(4 * b, 4 * b + 4):
                turned = recv2[d, pl.ds(z, HALF, stride=LZ), :].T
                parts.append(jnp.concatenate([turned[:LY], turned[LY:]], 1))
            lines = split(jnp.concatenate(parts, 0))
            out = dot3(lines, (x_out[0], x_out[1])) + drift
            velocity[0, d, 4 * b : 4 * b + 4] = out.reshape(4, LY, N)

    for c in range(3):
        wait_bytes(send.at[c, pl.ds(0, (PEERS - 1) * LZ)], ssem.at[c])
        wait_bytes(send.at[c, pl.ds(0, (PEERS - 1) * LZ)], ssem2.at[c])


def spectral_velocity(vorticity, wind):
    tables = [jnp.asarray(t) for t in make_tables()]
    vmem = pl.BlockSpec(memory_space=pltpu.VMEM)
    return pl.pallas_call(
        spectral_kernel,
        out_shape=jax.ShapeDtypeStruct(vorticity.shape, jnp.float32),
        in_specs=[vmem, pl.BlockSpec(memory_space=pltpu.SMEM)] + [vmem] * 5,
        out_specs=vmem,
        scratch_shapes=[
            pltpu.VMEM((3, PEERS * LZ, 128), jnp.float32),
            pltpu.VMEM((3, GY, N, 128), jnp.float32),
            pltpu.VMEM((3, 2, N, N), jnp.float32),
            pltpu.VMEM((3, GY, N, 128), jnp.float32),
            pltpu.VMEM((3, PEERS * LZ, 128), jnp.float32),
            pltpu.VMEM((2, N, N), jnp.float32),
            pltpu.SemaphoreType.DMA((3,)),
            pltpu.SemaphoreType.DMA((3,)),
            pltpu.SemaphoreType.DMA((3,)),
            pltpu.SemaphoreType.DMA((3,)),
        ],
        compiler_params=pltpu.CompilerParams(collective_id=0, has_side_effects=True),
    )(vorticity, wind, *tables)


def shifted(value, axis, steps):
    count = lax.axis_size(axis)
    initial, last = (max(0, -steps), min(count, count - steps))
    return lax.ppermute(value, axis, [(source, source + steps) for source in range(initial, last)])


def padded(array, sides, width):
    edges = {}
    for axis, dim in sides:
        devices, length = (lax.axis_size(axis), array.shape[dim])
        up = [(i, (i + 1) % devices) for i in range(devices)]
        last = lax.slice_in_dim(array, length - width, length, axis=dim)
        initial = lax.slice_in_dim(array, 0, width, axis=dim)
        edges[dim] = (
            lax.ppermute(last, axis, up),
            lax.ppermute(initial, axis, [(b, a) for a, b in up]),
        )
    done = []
    for _, dim in sides:
        low, high = edges[dim]
        around = [(width, width) if d in done else (0, 0) for d in range(array.ndim)]
        array = jnp.concatenate([jnp.pad(low, around), array, jnp.pad(high, around)], axis=dim)
        done.append(dim)
    return array


def extended_2(cells, sides, width):
    for axis, dim in sides:
        count = lax.axis_size(axis)
        head = lax.slice_in_dim(cells, 0, width, axis=dim)
        tail = lax.slice_in_dim(cells, cells.shape[dim] - width, cells.shape[dim], axis=dim)
        cells = jnp.concatenate(
            [
                lax.ppermute(tail, axis, [(i, (i + 1) % count) for i in range(count)]),
                cells,
                lax.ppermute(head, axis, [((i + 1) % count, i) for i in range(count)]),
            ],
            axis=dim,
        )
    return cells


def kernel_weight(offset):
    mag = jnp.abs(offset)
    inner = 1.0 - 2.5 * mag * mag + 1.5 * mag * mag * mag
    outer = 0.5 * (2.0 - mag) * (2.0 - mag) * (1.0 - mag)
    return jnp.where(mag < 1.0, inner, jnp.where(mag < 2.0, outer, 0.0 * mag))


def body(vorticity, wind):
    is_wake = lax.axis_index("grp") == 1
    velocity = spectral_velocity(vorticity, wind)[0]
    field = vorticity[0]
    count_x = field.shape[3]
    planes = shifted(velocity[..., count_x - 2 :], "grp", 1)
    rimmed = padded(velocity, (("gz", 1), ("gy", 2)), 1)
    grad_z = (rimmed[:, 2:, 1:-1, :] - rimmed[:, :-2, 1:-1, :]) * 0.5
    grad_y = (rimmed[:, 1:-1, 2:, :] - rimmed[:, 1:-1, :-2, :]) * 0.5
    left_side = jnp.where(is_wake, planes[..., 1:], velocity[..., count_x - 1 :])
    right_side = jnp.where(is_wake, velocity[..., count_x - 1 :], velocity[..., :1])
    extended = jnp.concatenate([left_side, velocity, right_side], -1)
    grad_x = (extended[..., 2:] - extended[..., :-2]) * 0.5
    strength = field + TIME_STEP * (field[0:1] * grad_x + field[1:2] * grad_y + field[2:3] * grad_z)
    ghost = shifted(strength[..., count_x - 2 :], "grp", 1)
    shift_x = TIME_STEP * velocity[0]
    left_q = jnp.where(is_wake, ghost, strength[..., count_x - 2 :])
    left_d = jnp.where(is_wake, TIME_STEP * planes[0], shift_x[..., count_x - 2 :])
    right_q = jnp.where(is_wake, 0.0, strength[..., :2])
    right_d = jnp.where(is_wake, 0.0, shift_x[..., :2])
    q_ext = jnp.concatenate([left_q, strength, right_q], -1)
    d_ext = jnp.concatenate([left_d, shift_x, right_d], -1)
    moved = jnp.zeros_like(strength)
    for offset in range(-2, 3):
        start = 2 - offset
        moved = moved + q_ext[..., start : start + count_x] * kernel_weight(
            offset - d_ext[..., start : start + count_x]
        )
    packed = jnp.concatenate([moved, TIME_STEP * velocity[1:2]], 0)
    rim_rows = extended_2(packed, (("gy", 2),), 2)
    width_y = moved.shape[2]
    lateral = jnp.zeros_like(moved)
    for offset in range(-2, 3):
        start = 2 - offset
        lateral = lateral + rim_rows[:3, :, start : start + width_y, :] * kernel_weight(
            offset - rim_rows[3:4, :, start : start + width_y, :]
        )
    packed = jnp.concatenate([lateral, TIME_STEP * velocity[2:3]], 0)
    rim_cols = extended_2(packed, (("gz", 1),), 2)
    width_z = moved.shape[1]
    result = jnp.zeros_like(moved)
    for offset in range(-2, 3):
        start = 2 - offset
        result = result + rim_cols[:3, start : start + width_z, :, :] * kernel_weight(
            offset - rim_cols[3:4, start : start + width_z, :, :]
        )
    return (result[None], velocity[None])


def solution(mesh):
    return jax.shard_map(
        body,
        mesh=mesh,
        in_specs=(P("grp", None, "gz", "gy", None), P("grp", None)),
        out_specs=(P("grp", None, "gz", "gy", None), P("grp", None, "gz", "gy", None)),
        check_vma=False,
    )
```

profile of v0, /device:TPU:0, one launch (start us, length us, event | category | flops | bytes accessed | tf_op | source)
XLA Modules:
  0.0 161.5 jit_solution(11492125723204584580)
XLA Ops:
  0.6 83.0 %shard_map.86 = f32[1,3,8,64,256]{4,3,2,1,0:T(8,128)} custom-call(f32[1,3,8,64,256]{4,3,2,1,0:T(8,128)} %field.1, f32[1,3]{1,0:T(1,128)} %wind.1, bf16[2,256,256]{2,1,0:T(8,128)(2,1)} %constant.29.clone.x_in, bf16[2,512,512]{2,1,0:T(8,128)(2,1)} %constant.30.clone.y_in, bf16[2,2,256,256]{3,2,1,0:T(8,128)(2,1)} %constant.8.clone.z_all, ...), custom_call_target="tpu_custom_call" | custom-call | tf_op jit(solution)/shard_map/pallas_call | solution.py:233
  84.7 1.7 %collective-permute-start.3 = (f32[3,8,1,256]{3,2,1,0:T(1,128)S(1)}, f32[3,8,1,256]{3,2,1,0:T(1,128)S(1)}, u32[]{:S(2)}, u32[]{:S(2)}) collective-permute-start(f32[3,8,1,256]{3,2,1,0:T(1,128)S(1)} %get-tuple-element.35), channel_id=1, source_target_pairs={{32,0},{64,32},{96,64},{0,96},{33,1},{65,33},{97,65},{1,97},{34,2}... | collective-permute-start | bytes 73736 | tf_op jit(solution)/shard_map/ppermute | solution.py:269
  86.9 1.8 %fusion.135 = (f32[3,1,64,256]{3,2,1,0:T(8,128)}, f32[3,1,64,256]{3,2,1,0:T(8,128)}) fusion(f32[3,8,64,256]{3,2,1,0:T(8,128)} %bitcast.72), kind=kLoop, calls=%fused_computation.251 | loop fusion | bytes 786432 | tf_op jit(solution)/shard_map/slice | solution.py:266
  88.7 3.2 %collective-permute-start.2 = (f32[3,1,64,256]{3,2,1,0:T(8,128)}, f32[3,1,64,256]{3,2,1,0:T(8,128)}, u32[]{:S(2)}, u32[]{:S(2)}) collective-permute-start(f32[3,1,64,256]{3,2,1,0:T(8,128)} %get-tuple-element.37), channel_id=1, source_target_pairs={{1,0},{2,1},{3,2},{4,3},{5,4},{6,5},{7,6},{8,7},{9,8},{10,9},{11,1... | collective-permute-start | bytes 589832 | tf_op jit(solution)/shard_map/ppermute | solution.py:269
  91.9 1.4 slice.252
  93.6 6.5 %collective-permute-start = (f32[3,8,64,2]{2,1,3,0:T(8,128)S(1)}, f32[3,8,64,2]{2,1,3,0:T(8,128)S(1)}, u32[]{:S(2)}, u32[]{:S(2)}) collective-permute-start(f32[3,8,64,2]{2,1,3,0:T(8,128)S(1)} %copy.9), channel_id=1, source_target_pairs={{0,128},{1,129},{2,130},{3,131},{4,132},{5,133},{6,134},{7,135},{8... | collective-permute-start | bytes 36872 | tf_op jit(solution)/shard_map/ppermute | solution.py:257
  100.2 1.2 multiply_bitcast_fusion.3
  101.4 1.1 multiply_bitcast_fusion
  105.0 3.0 %fusion.23 = f32[3,8,64,256]{3,2,1,0:T(8,128)S(1)} fusion(f32[3,8,64,256]{3,2,1,0:T(8,128)S(1)} %bitcast.75, f32[3,1,64,256]{3,2,1,0:T(8,128)} %collective-permute-done.1, f32[3,1,64,256]{3,2,1,0:T(8,128)} %collective-permute-done.2, f32[3,8,1,256]{3,2,1,0:T(1,128)S(1)} %collective-permute-done.4, f32[3,8,1,256]{3,2,1,0:T(1,128)S(1)} %collective-permute-done.3, ...), kind=kLoop, calls=%fused_computation.42 | loop fusion | flops 10223616 | bytes 6746112 | tf_op jit(solution)/shard_map/add | solution.py:316
  108.0 1.2 slice.264
  109.2 1.4 copy.11
  110.6 7.3 %collective-permute-start.5 = (f32[3,8,64,2]{2,1,3,0:T(8,128)S(1)}, f32[3,8,64,2]{2,1,3,0:T(8,128)S(1)}, u32[]{:S(2)}, u32[]{:S(2)}) collective-permute-start(f32[3,8,64,2]{2,1,3,0:T(8,128)S(1)} %copy.11), channel_id=1, source_target_pairs={{0,128},{1,129},{2,130},{3,131},{4,132},{5,133},{6,134},{7,135},{8... | collective-permute-start | bytes 36872 | tf_op jit(solution)/shard_map/ppermute | solution.py:257
  117.9 5.2 %fusion.33 = (f32[8,64,256]{2,1,0:T(8,128)}, f32[8,64,256]{2,1,0:T(8,128)}, f32[8,64,256]{2,1,0:T(8,128)}, f32[8,64,256]{2,1,0:T(8,128)}, f32[8,64,256]{2,1,0:T(...) fusion(f32[8,64,2]{2,1,0:T(8,128)S(1)} %get-tuple-element.45, f32[8,64,256]{2,1,0:T(8,128)} %copy-done.5, ...), kind=kLoop, calls=%fused_computation.115 | loop fusion | flops 18350080 | bytes 5775360 | tf_op jit(solution)/shard_map/jit(_where)/select_n | solution.py:300
  123.1 1.2 copy.12
  126.0 2.6 %fusion.3 = f32[3,8,64,256]{3,2,1,0:T(8,128)S(1)} fusion(f32[3,8,64,2]{3,2,1,0:T(8,128)S(1)} %get-tuple-element.29, f32[3,8,64,256]{3,2,1,0:T(8,128)S(1)} %fusion.23, f32[3,8,64,2]{3,2,1,0:T(8,128)S(1)} %get-tuple-element.28, f32[8,64,256]{2,1,0:T(8,128)S(1)} %copy-done.8, f32[8,64,256]{2,1,0:T(8,128)S(1)} %copy-done.9, f32[8,64,256]{2,1,0:T(8,128)S(1)} %copy-done.10, ...), kind=kLoop, calls=%fused_computation.11 | loop fusion | flops 5111808 | bytes 5791744 | tf_op jit(solution)/shard_map/add | solution.py:328
  128.7 3.5 %collective-permute-start.6 = (f32[4,8,2,256]{3,2,1,0:T(2,128)S(1)}, f32[4,8,2,256]{3,2,1,0:T(2,128)S(1)}, u32[]{:S(2)}, u32[]{:S(2)}) collective-permute-start(f32[4,8,2,256]{3,2,1,0:T(2,128)S(1)} %get-tuple-element.20), channel_id=1, source_target_pairs={{32,0},{64,32},{96,64},{0,96},{33,1},{65,33},{97,65},{1,97},{34,2}... | collective-permute-start | bytes 196616 | tf_op jit(solution)/shard_map/ppermute | solution.py:289
  132.2 1.9 %collective-permute-done.6 = f32[4,8,2,256]{3,2,1,0:T(2,128)S(1)} collective-permute-done((f32[4,8,2,256]{3,2,1,0:T(2,128)S(1)}, f32[4,8,2,256]{3,2,1,0:T(2,128)S(1)}, u32[]{:S(2)}, u32[]{:S(2)}) %collective-permute-start.6) | collective-permute-done | bytes 65568 | tf_op jit(solution)/shard_map/ppermute | solution.py:289
  134.1 4.2 %collective-permute-done.7 = f32[4,8,2,256]{3,2,1,0:T(2,128)S(1)} collective-permute-done((f32[4,8,2,256]{3,2,1,0:T(2,128)S(1)}, f32[4,8,2,256]{3,2,1,0:T(2,128)S(1)}, u32[]{:S(2)}, u32[]{:S(2)}) %collective-permute-start.7) | collective-permute-done | bytes 65568 | tf_op jit(solution)/shard_map/ppermute | solution.py:287
  138.3 1.4 fusion.59
  141.9 2.3 %collective-permute-start.8 = (f32[4,2,64,256]{3,2,1,0:T(8,128)S(1)}, f32[4,2,64,256]{3,2,1,0:T(8,128)S(1)}, u32[]{:S(2)}, u32[]{:S(2)}) collective-permute-start(f32[4,2,64,256]{3,2,1,0:T(8,128)S(1)} %get-tuple-element.14), channel_id=1, source_target_pairs={{1,0},{2,1},{3,2},{4,3},{5,4},{6,5},{7,6},{8,7},{9,8},{10,9},{11,1... | collective-permute-start | bytes 1572872 | tf_op jit(solution)/shard_map/ppermute | solution.py:289
  144.2 6.7 %collective-permute-done.8 = f32[4,2,64,256]{3,2,1,0:T(8,128)S(1)} collective-permute-done((f32[4,2,64,256]{3,2,1,0:T(8,128)S(1)}, f32[4,2,64,256]{3,2,1,0:T(8,128)S(1)}, u32[]{:S(2)}, u32[]{:S(2)}) %collective-permute-start.8) | collective-permute-done | bytes 524320 | tf_op jit(solution)/shard_map/ppermute | solution.py:289
  150.9 5.2 %collective-permute-done.9 = f32[4,2,64,256]{3,2,1,0:T(8,128)S(1)} collective-permute-done((f32[4,2,64,256]{3,2,1,0:T(8,128)S(1)}, f32[4,2,64,256]{3,2,1,0:T(8,128)S(1)}, u32[]{:S(2)}, u32[]{:S(2)}) %collective-permute-start.9) | collective-permute-done | bytes 524320 | tf_op jit(solution)/shard_map/ppermute | solution.py:287
  156.1 1.3 fusion.88
  158.4 1.9 %fusion.9 = f32[1,3,8,64,256]{4,3,2,1,0:T(8,128)} fusion(f32[4,10,64,256]{3,2,1,0:T(8,128)S(1)} %get-tuple-element.13, f32[4,10,64,256]{3,2,1,0:T(8,128)S(1)} %get-tuple-element.12, f32[3,8,64,256]{3,2,1,0:T(8,128)S(1)} %fusion.13, f32[8,64,256]{2,1,0:T(8,128)S(1)} %get-tuple-element.10, f32[8,64,256]{2,1,0:T(8,128)S(1)} %get-tuple-element.11, ...), kind=kLoop, calls=%fused_computation.18 | loop fusion | flops 3538944 | bytes 12058624 | tf_op jit(solution)/shard_map/broadcast_in_dim | solution.py:349
  (57 shorter events, 10.3 us)
Async XLA Ops:
  84.7 19.5 %collective-permute-start.3 = (f32[3,8,1,256]{3,2,1,0:T(1,128)S(1)}, f32[3,8,1,256]{3,2,1,0:T(1,128)S(1)}, u32[]{:S(2)}, u32[]{:S(2)}) collective-permute-start(f32[3,8,1,256]{3,2,1,0:T(1,128)S(1)} %get-tuple-element.35), channel_id=1, source_target_pairs={{32,0},{64,32},{96,64},{0,96},{33,1},{65,33},{97,65},{1,97},{34,2}... | collective-permute-start | bytes 73736 | tf_op jit(solution)/shard_map/ppermute | solution.py:269
  86.4 13.8 %copy-start.1 = (f32[1,3,8,64,256]{4,3,2,1,0:T(8,128)S(1)}, f32[1,3,8,64,256]{4,3,2,1,0:T(8,128)}, u32[]{:S(2)}) copy-start(f32[1,3,8,64,256]{4,3,2,1,0:T(8,128)} %field.1) | copy-start | bytes 4718596
  86.4 17.8 %collective-permute-start.4 = (f32[3,8,1,256]{3,2,1,0:T(1,128)S(1)}, f32[3,8,1,256]{3,2,1,0:T(1,128)S(1)}, u32[]{:S(2)}, u32[]{:S(2)}) collective-permute-start(f32[3,8,1,256]{3,2,1,0:T(1,128)S(1)} %get-tuple-element.36), channel_id=1, source_target_pairs={{0,32},{32,64},{64,96},{96,0},{1,33},{33,65},{65,97},{97,1},{2,34}... | collective-permute-start | bytes 73736 | tf_op jit(solution)/shard_map/ppermute | solution.py:268
  88.7 15.6 %collective-permute-start.2 = (f32[3,1,64,256]{3,2,1,0:T(8,128)}, f32[3,1,64,256]{3,2,1,0:T(8,128)}, u32[]{:S(2)}, u32[]{:S(2)}) collective-permute-start(f32[3,1,64,256]{3,2,1,0:T(8,128)} %get-tuple-element.37), channel_id=1, source_target_pairs={{1,0},{2,1},{3,2},{4,3},{5,4},{6,5},{7,6},{8,7},{9,8},{10,9},{11,1... | collective-permute-start | bytes 589832 | tf_op jit(solution)/shard_map/ppermute | solution.py:269
  91.9 12.3 %collective-permute-start.1 = (f32[3,1,64,256]{3,2,1,0:T(8,128)}, f32[3,1,64,256]{3,2,1,0:T(8,128)}, u32[]{:S(2)}, u32[]{:S(2)}) collective-permute-start(f32[3,1,64,256]{3,2,1,0:T(8,128)} %get-tuple-element.38), channel_id=1, source_target_pairs={{0,1},{1,2},{2,3},{3,4},{4,5},{5,6},{6,7},{7,8},{8,9},{9,10},{10,1... | collective-permute-start | bytes 589832 | tf_op jit(solution)/shard_map/ppermute | solution.py:268
  93.6 7.8 %copy-start = (f32[1,3,8,64,256]{4,3,2,1,0:T(8,128)S(1)}, f32[1,3,8,64,256]{4,3,2,1,0:T(8,128)}, u32[]{:S(2)}) copy-start(f32[1,3,8,64,256]{4,3,2,1,0:T(8,128)} %shard_map.86) | copy-start | bytes 4718596
  93.6 8.9 %collective-permute-start = (f32[3,8,64,2]{2,1,3,0:T(8,128)S(1)}, f32[3,8,64,2]{2,1,3,0:T(8,128)S(1)}, u32[]{:S(2)}, u32[]{:S(2)}) collective-permute-start(f32[3,8,64,2]{2,1,3,0:T(8,128)S(1)} %copy.9), channel_id=1, source_target_pairs={{0,128},{1,129},{2,130},{3,131},{4,132},{5,133},{6,134},{7,135},{8... | collective-permute-start | bytes 36872 | tf_op jit(solution)/shard_map/ppermute | solution.py:257
  103.0 1.4 copy-start.2
  103.0 1.6 copy-start.15
  103.4 1.5 copy-start.13
  103.4 1.7 %copy-start.14 = (f32[8,64,256]{2,1,0:T(8,128)S(1)}, f32[8,64,256]{2,1,0:T(8,128)}, u32[]{:S(2)}) copy-start(f32[8,64,256]{2,1,0:T(8,128)} %get-tuple-element.31) | copy-start | bytes 1572868
  110.6 12.5 %collective-permute-start.5 = (f32[3,8,64,2]{2,1,3,0:T(8,128)S(1)}, f32[3,8,64,2]{2,1,3,0:T(8,128)S(1)}, u32[]{:S(2)}, u32[]{:S(2)}) collective-permute-start(f32[3,8,64,2]{2,1,3,0:T(8,128)S(1)} %copy.11), channel_id=1, source_target_pairs={{0,128},{1,129},{2,130},{3,131},{4,132},{5,133},{6,134},{7,135},{8... | collective-permute-start | bytes 36872 | tf_op jit(solution)/shard_map/ppermute | solution.py:257
  124.3 1.0 copy-start.6
  124.3 1.2 copy-start.7
  124.3 1.4 copy-start.8
  124.3 1.5 copy-start.9
  124.3 1.7 %copy-start.10 = (f32[8,64,256]{2,1,0:T(8,128)S(1)}, f32[8,64,256]{2,1,0:T(8,128)}, u32[]{:S(2)}) copy-start(f32[8,64,256]{2,1,0:T(8,128)} %get-tuple-element.48) | copy-start | bytes 1572868
  126.0 2.6 %copy-start.4 = (f32[1,8,64,256]{3,2,1,0:T(8,128)S(1)}, f32[1,8,64,256]{3,2,1,0:T(8,128)}, u32[]{:S(2)}) copy-start(f32[1,8,64,256]{3,2,1,0:T(8,128)} %get-tuple-element.27) | copy-start | bytes 1572868
  128.7 5.4 %collective-permute-start.6 = (f32[4,8,2,256]{3,2,1,0:T(2,128)S(1)}, f32[4,8,2,256]{3,2,1,0:T(2,128)S(1)}, u32[]{:S(2)}, u32[]{:S(2)}) collective-permute-start(f32[4,8,2,256]{3,2,1,0:T(2,128)S(1)} %get-tuple-element.20), channel_id=1, source_target_pairs={{32,0},{64,32},{96,64},{0,96},{33,1},{65,33},{97,65},{1,97},{34,2}... | collective-permute-start | bytes 196616 | tf_op jit(solution)/shard_map/ppermute | solution.py:289
  132.2 6.1 %collective-permute-start.7 = (f32[4,8,2,256]{3,2,1,0:T(2,128)S(1)}, f32[4,8,2,256]{3,2,1,0:T(2,128)S(1)}, u32[]{:S(2)}, u32[]{:S(2)}) collective-permute-start(f32[4,8,2,256]{3,2,1,0:T(2,128)S(1)} %get-tuple-element.21), channel_id=1, source_target_pairs={{0,32},{32,64},{64,96},{96,0},{1,33},{33,65},{65,97},{97,1},{2,34}... | collective-permute-start | bytes 196616 | tf_op jit(solution)/shard_map/ppermute | solution.py:287
  139.7 1.0 copy-start.12
  141.9 9.0 %collective-permute-start.8 = (f32[4,2,64,256]{3,2,1,0:T(8,128)S(1)}, f32[4,2,64,256]{3,2,1,0:T(8,128)S(1)}, u32[]{:S(2)}, u32[]{:S(2)}) collective-permute-start(f32[4,2,64,256]{3,2,1,0:T(8,128)S(1)} %get-tuple-element.14), channel_id=1, source_target_pairs={{1,0},{2,1},{3,2},{4,3},{5,4},{6,5},{7,6},{8,7},{9,8},{10,9},{11,1... | collective-permute-start | bytes 1572872 | tf_op jit(solution)/shard_map/ppermute | solution.py:289
  144.2 11.9 %collective-permute-start.9 = (f32[4,2,64,256]{3,2,1,0:T(8,128)S(1)}, f32[4,2,64,256]{3,2,1,0:T(8,128)S(1)}, u32[]{:S(2)}, u32[]{:S(2)}) collective-permute-start(f32[4,2,64,256]{3,2,1,0:T(8,128)S(1)} %get-tuple-element.15), channel_id=1, source_target_pairs={{0,1},{1,2},{2,3},{3,4},{4,5},{5,6},{6,7},{7,8},{8,9},{9,10},{10,1... | collective-permute-start | bytes 1572872 | tf_op jit(solution)/shard_map/ppermute | solution.py:287
  157.4 1.0 copy-start.11
  (2 other events, 1.9 us)
where the time goes:
time: 162 us
  Pallas kernels  83 us (51%)
  starting transfers between devices  24.9 us (15%)
  other arithmetic  21.6 us (13%)
  waiting for transfers between devices  18 us (11%)
  local copies, waits for them, and re-layouts  13.1 us (8%)
    pallas_call x1, Pallas kernels, spectral_velocity(): pl.pallas_call(spectral_kernel, out_shape=jax.ShapeDtypeStruct(vorticity....  83 us
    ppermute x2, starting transfers between devices, shifted(): lax.ppermute(value, axis, [(source, source + steps) for source in range(i...  13.8 us
    ppermute x2, waiting for transfers between devices, extended_2(): lax.ppermute(tail, axis, [(i, (i + 1) % count) for i in range(count)])  9.38 us
    ppermute x2, waiting for transfers between devices, extended_2(): lax.ppermute(head, axis, [((i + 1) % count, i) for i in range(count)])  8.6 us
    ppermute x2, starting transfers between devices, extended_2(): lax.ppermute(head, axis, [((i + 1) % count, i) for i in range(count)])  5.78 us
    select_n x1, other arithmetic, kernel_weight(): return jnp.where(mag < 1.0, inner, jnp.where(mag < 2.0, outer, 0.0 * mag))  5.23 us
    ppermute x2, starting transfers between devices, padded(): lax.ppermute(initial, axis, [(b, a) for a, b in up])  4.91 us
    unnamed x33, local copies, waits for them, and re-layouts  4.28 us
  transfers between devices with their start and end apart: 10, of which 4 were waited for; matrix products, arithmetic and copies ran while one was open for 8% of the time, Pallas kernels for 0%

commit v1 on v0

v1 whole, which is shorter than its diff:
```python
import functools
import math

import jax
import jax.numpy as jnp
import numpy as np
from jax import lax
from jax.experimental import pallas as pl
from jax.experimental.pallas import tpu as pltpu
from jax.sharding import PartitionSpec as P

TIME_STEP = 0.4
MESH = pl.DeviceIdType.MESH
N = 256
HALF = 128
GY = 4
GZ = 32
PEERS = GY * GZ
LZ = 8
LY = 64


def split(values):
    high = values.astype(jnp.bfloat16)
    low = (values - high.astype(jnp.float32)).astype(jnp.bfloat16)
    return high, low


def table_pair(table):
    table = np.asarray(table, np.float32)
    high = table.astype(jnp.bfloat16)
    low = (table - high.astype(np.float32)).astype(jnp.bfloat16)
    return np.stack([high, low])


def make_tables():
    index = np.arange(N)
    angle = (index[:, None] * index[None, :] % N) * (2.0 * math.pi / N)
    cosine, sine = np.cos(angle), np.sin(angle)
    alternate = 1.0 - 2.0 * (index % 2)
    sine_in = -sine[:HALF].copy()
    sine_in[0] = alternate
    x_in = np.concatenate([cosine[:HALF], sine_in], 0)
    x_out = 2.0 * x_in / N
    x_out[0] *= 0.5
    x_out[HALF] *= 0.5
    cos_y = cosine.reshape(GY, 1, LY, N)
    sin_y = sine.reshape(GY, 1, LY, N)
    to_real = np.concatenate([cos_y, sin_y], 1).reshape(2 * N, N)
    to_imag = np.concatenate([-sin_y, cos_y], 1).reshape(2 * N, N)
    y_in = np.concatenate([to_real, to_imag], 1)
    y_out = np.concatenate([to_real, to_imag], 1).T / N
    z_all = np.stack([cosine, sine])
    return [table_pair(t) for t in (x_in, y_in, z_all, y_out, x_out)]


def dot3(a, b, dims=((1,), (0,))):
    def one(left, right):
        return lax.dot_general(left, right, (dims, ((), ())), preferred_element_type=jnp.float32)

    return one(a[0], b[0]) + (one(a[0], b[1]) + one(a[1], b[0]))


def each_peer(gy, gz, visit):
    for q in range(1, GY):
        visit(lax.rem(gy + q, GY), gz)

    def step(k, carry):
        other_z = lax.rem(gz + k, GZ)
        for q in range(GY):
            visit(lax.rem(gy + q, GY), other_z)
        return carry

    lax.fori_loop(1, GZ, step, 0)


def wait_bytes(ref, sem):
    pltpu.make_async_copy(ref, ref, sem).wait()


def waves(shape, axis):
    index = lax.broadcasted_iota(jnp.int32, shape, axis)
    signed = jnp.where(index < N // 2, index, index - N)
    full = signed.astype(jnp.float32) * (2.0 * math.pi / N)
    return full, jnp.where(index == N // 2, 0.0, full)


def kernel_weight(offset):
    mag = jnp.abs(offset)
    square = mag * mag
    inner = 1.0 + square * (1.5 * mag - 2.5)
    rest = 2.0 - mag
    outer = 0.5 * rest * rest * (1.0 - mag)
    return jnp.where(mag < 1.0, inner, jnp.where(mag < 2.0, outer, 0.0 * mag))


def moved_by(values, steps, axis):
    return pltpu.roll(values, steps % values.shape[axis], axis)


def step_kernel(
    field, wind, x_in, y_in, z_all, y_out, x_out, result_out, velocity_out,
    send, recv, stream, send2, recv2, scale, speed, weight_x, weight_y, weight_z,
    moved, result, row_out, row_in, column_out, column_in, ghost_out, ghost_in,
    lateral_out, lateral_in, layer_out, layer_in,
    ssem, rsem, ssem2, rsem2, plane_s, plane_r, row_s, row_r, column_s, column_r,
    ghost_s, ghost_r, lateral_s, lateral_r, layer_s, layer_r, store_s,
):
    grp = lax.axis_index("grp")
    gy = lax.axis_index("gy")
    gz = lax.axis_index("gz")
    me = gy * GZ + gz
    is_wake = grp == 1
    next_y, last_y = lax.rem(gy + 1, GY), lax.rem(gy + GY - 1, GY)
    next_z, last_z = lax.rem(gz + 1, GZ), lax.rem(gz + GZ - 1, GZ)
    barrier = pltpu.get_barrier_semaphore()

    def remote(source, target, sems, device):
        pltpu.make_async_remote_copy(
            source, target, sems[0], sems[1], device_id=device, device_id_type=MESH
        ).start()

    def greet(other_y, other_z):
        pl.semaphore_signal(
            barrier, inc=1, device_id={"gy": other_y, "gz": other_z}, device_id_type=MESH
        )

    each_peer(gy, gz, greet)
    pl.semaphore_signal(barrier, inc=1, device_id={"grp": 1 - grp}, device_id_type=MESH)

    lane = lax.broadcasted_iota(jnp.int32, (HALF, 128), 1)
    first_half = lane < LY
    for c in (1, 2, 0):
        for b in range(2):
            rows = field[0, c, 4 * b : 4 * b + 4].reshape(4 * LY, N)
            lines = dot3((x_in[0], x_in[1]), split(rows), ((1,), (1,)))
            for t in range(2):
                real = lines[:HALF, 128 * t : 128 * t + 128]
                imag = lines[HALF:, 128 * t : 128 * t + 128]
                even = jnp.where(first_half, real, pltpu.roll(imag, LY, 1))
                odd = jnp.where(first_half, pltpu.roll(real, LY, 1), imag)
                z = 4 * b + 2 * t
                send[c, pl.ds(z, HALF, stride=LZ), :] = even
                send[c, pl.ds(z + 1, HALF, stride=LZ), :] = odd
    mine = pl.ds(pl.multiple_of(me * LZ, LZ), LZ)
    mine_z = pl.ds(pl.multiple_of(gz * LZ, LZ), LZ)
    pl.semaphore_wait(barrier, PEERS)

    for c in (1, 2, 0):
        def out(other_y, other_z, c=c):
            other = other_y * GZ + other_z
            remote(
                send.at[c, pl.ds(pl.multiple_of(other * LZ, LZ), LZ)],
                recv.at[c, gy, mine_z],
                (ssem.at[c], rsem.at[c]),
                {"gy": other_y, "gz": other_z},
            )

        each_peer(gy, gz, out)
        recv[c, gy, mine_z, :] = send[c, mine, :]

    wave_z, curl_z = waves((N, N), 0)
    wave_y, curl_y = waves((N, N), 1)
    curl_x = me.astype(jnp.float32) * (2.0 * math.pi / N)
    squared = curl_x * curl_x + wave_y * wave_y + wave_z * wave_z
    positive = squared > 0
    scale[0] = jnp.where(positive, 1.0 / jnp.where(positive, squared, 1.0), 0.0)

    @pl.when(me == 0)
    def _():
        base = scale[0]
        top = 1.0 / (squared + math.pi * math.pi)
        scale[0] = 0.5 * (base + top)
        scale[1] = 0.5 * (base - top)

    curl = (curl_x, curl_y, curl_z)
    table_y = (y_in[0], y_in[1])
    cosine = (z_all[0, 0], z_all[1, 0])
    sine = (z_all[0, 1], z_all[1, 1])

    def transform(plane):
        lines = split(dot3(split(plane), table_y))
        by_cos = dot3(cosine, lines)
        by_sin = dot3(sine, lines)
        real = by_cos[:, :N] + by_sin[:, N:]
        imag = by_cos[:, N:] - by_sin[:, :N]
        return real, imag

    def forward(c):
        wait_bytes(recv2.at[c, pl.ds(0, (PEERS - 1) * LZ)], rsem.at[c])
        plane = jnp.concatenate([recv[c, j] for j in range(GY)], 1)
        real, imag = transform(plane)
        stream[c, 0] = real * scale[0]
        stream[c, 1] = imag * scale[0]

        @pl.when(me == 0)
        def _():
            column = lax.broadcasted_iota(jnp.int32, (N, 2 * N), 1)
            plane = jnp.concatenate([recv[c, j] for j in range(GY)], 1)
            real, imag = transform(jnp.where(column % 128 < LY, plane, -plane))
            stream[c, 0] += real * scale[1]
            stream[c, 1] += imag * scale[1]

    def backward(d):
        a, b = (d + 1) % 3, (d + 2) % 3
        real = curl[b] * stream[a, 1] - curl[a] * stream[b, 1]
        imag = curl[a] * stream[b, 0] - curl[b] * stream[a, 0]
        lines = split(jnp.concatenate([real, imag], 1))
        by_cos = dot3(cosine, lines)
        by_sin = dot3(sine, lines)
        real = by_cos[:, :N] - by_sin[:, N:]
        imag = by_cos[:, N:] + by_sin[:, :N]
        lines = split(jnp.concatenate([real, imag], 1) * (1.0 / N))
        plane = dot3(lines, (y_out[0], y_out[1]))
        for j in range(GY):
            send2[d, j] = plane[:, 128 * j : 128 * j + 128]

        def out(other_y, other_z):
            remote(
                send2.at[d, other_y, pl.ds(pl.multiple_of(other_z * LZ, LZ), LZ)],
                recv2.at[d, mine],
                (ssem2.at[d], rsem2.at[d]),
                {"gy": other_y, "gz": other_z},
            )

        each_peer(gy, gz, out)
        recv2[d, mine, :] = send2[d, gy, mine_z, :]

    forward(1)
    forward(2)
    backward(0)
    forward(0)
    backward(1)
    backward(2)

    row = lax.broadcasted_iota(jnp.int32, (LY, N), 0)
    column = lax.broadcasted_iota(jnp.int32, (LY, N), 1)
    tile = lax.broadcasted_iota(jnp.int32, (LY, 128), 1)
    short_row = lax.broadcasted_iota(jnp.int32, (8, N), 0)
    no_wrap_low = jnp.where(is_wake, 0, -N)
    no_wrap_high = jnp.where(is_wake, N, 2 * N)
    first_column = jnp.where(is_wake, 0, -1)
    last_column = jnp.where(is_wake, N - 1, N)

    def velocity_of(d):
        wait_bytes(recv.at[0, :, pl.ds(0, (PEERS - 1) * LZ // GY)], rsem2.at[d])
        drift = wind[0, d]
        edge = jnp.zeros((LY, 128), jnp.float32)
        for b in range(2):
            parts = []
            for z in range(4 * b, 4 * b + 4):
                turned = recv2[d, pl.ds(z, HALF, stride=LZ), :].T
                parts.append(jnp.concatenate([turned[:LY], turned[LY:]], 1))
            lines = split(jnp.concatenate(parts, 0))
            out = dot3(lines, (x_out[0], x_out[1])) + drift
            for z in range(4 * b, 4 * b + 4):
                plane = out[LY * (z - 4 * b) : LY * (z - 4 * b) + LY]
                speed[d, z + 1] = plane
                row_out[0, d * LZ + z : d * LZ + z + 1, :] = plane[LY - 1 :]
                row_out[1, d * LZ + z : d * LZ + z + 1, :] = plane[:1]
                edge = jnp.where(tile == z, pltpu.roll(plane[:, 128:], z + 1, 1), edge)
        column_out[d] = edge
        rows = pl.ds(d * LZ, LZ)
        remote(speed.at[d, LZ], speed.at[d, 0], (plane_s.at[d], plane_r.at[d]), {"gz": next_z})
        remote(speed.at[d, 1], speed.at[d, LZ + 1], (plane_s.at[d], plane_r.at[d]), {"gz": last_z})
        remote(row_out.at[0, rows], row_in.at[0, rows], (row_s.at[d], row_r.at[d]), {"gy": next_y})
        remote(row_out.at[1, rows], row_in.at[1, rows], (row_s.at[d], row_r.at[d]), {"gy": last_y})

        @pl.when(grp == 0)
        def _():
            remote(column_out.at[d], column_in.at[d], (column_s.at[d], column_r.at[d]), {"grp": 1})

        pltpu.make_async_copy(
            speed.at[d, pl.ds(1, LZ)], velocity_out.at[0, d], store_s.at[d]
        ).start()

    def weights(target, d):
        def at(z, carry):
            shift = TIME_STEP * speed[d, z + 1]
            for offset in range(-2, 3):
                value = kernel_weight(offset - shift)
                if d == 0 and offset > 0:
                    value = jnp.where(column >= no_wrap_high - offset, 0.0, value)
                if d == 0 and offset < 0:
                    value = jnp.where(column < no_wrap_low - offset, 0.0, value)
                target[offset + 2, z] = value
            return carry

        lax.fori_loop(0, LZ, at, 0)

    def stretch(d):
        wait_bytes(speed.at[d, pl.ds(0, 2)], plane_r.at[d])
        wait_bytes(row_in.at[0, pl.ds(0, 2 * LZ)], row_r.at[d])

        @pl.when(is_wake)
        def _():
            wait_bytes(column_in.at[d], column_r.at[d])

        def at(z, ghost):
            here = speed[d, z + 1]
            grad_z = speed[d, z + 2] - speed[d, z]
            low = row_in[0, pl.ds(d * LZ + z, 1), :]
            high = row_in[1, pl.ds(d * LZ + z, 1), :]
            up = jnp.where(row == LY - 1, high, moved_by(here, -1, 0))
            down = jnp.where(row == 0, low, moved_by(here, 1, 0))
            inflow = pltpu.roll(column_in[d], lax.rem(128 - z, 128), 1)
            left = moved_by(here, 1, 1)
            left = jnp.concatenate(
                [jnp.where(tile == first_column, inflow, left[:, :128]), left[:, 128:]], 1
            )
            right = jnp.where(column == last_column, here, moved_by(here, -1, 1))
            strength = field[0, d, z] + (0.5 * TIME_STEP) * (
                field[0, 0, z] * (right - left)
                + field[0, 1, z] * (up - down)
                + field[0, 2, z] * grad_z
            )
            one = moved_by(strength * weight_x[3, z], 1, 1)
            two = moved_by(strength * weight_x[4, z], 2, 1)
            total = strength * weight_x[2, z] + one + two
            total = total + moved_by(strength * weight_x[1, z], -1, 1)
            moved[d, z] = total + moved_by(strength * weight_x[0, z], -2, 1)
            over = jnp.where(tile == 0, one[:, :128], 0.0) + jnp.where(tile < 2, two[:, :128], 0.0)
            return ghost + pltpu.roll(over, 2 * z, 1)

        ghost_out[d] = lax.fori_loop(0, LZ, at, jnp.zeros((LY, 128), jnp.float32))

        @pl.when(grp == 0)
        def _():
            remote(ghost_out.at[d], ghost_in.at[d], (ghost_s.at[d], ghost_r.at[d]), {"grp": 1})

    def lateral_send(d):
        @pl.when(is_wake)
        def _():
            wait_bytes(ghost_in.at[d], ghost_r.at[d])

            def add(z, carry):
                inflow = pltpu.roll(ghost_in[d], lax.rem(128 - 2 * z, 128), 1)
                moved[d, z, :, :128] += jnp.where(tile < 2, inflow, 0.0)
                return carry

            lax.fori_loop(0, LZ, add, 0)

        def at(z, carry):
            here = moved[d, z]
            one = moved_by(here * weight_y[3, z], 1, 0)
            two = moved_by(here * weight_y[4, z], 2, 0)
            back_one = moved_by(here * weight_y[1, z], -1, 0)
            back_two = moved_by(here * weight_y[0, z], -2, 0)
            total = here * weight_y[2, z]
            total = total + jnp.where(row < 1, 0.0, one) + jnp.where(row < 2, 0.0, two)
            total = total + jnp.where(row >= LY - 1, 0.0, back_one)
            moved[d, z] = total + jnp.where(row >= LY - 2, 0.0, back_two)
            at_z = pl.ds(d * LZ + z, 1)
            lateral_out[0, 0, at_z, :] = one[0:1] + two[0:1]
            lateral_out[0, 1, at_z, :] = two[1:2]
            lateral_out[1, 0, at_z, :] = back_two[LY - 2 : LY - 1]
            lateral_out[1, 1, at_z, :] = back_one[LY - 1 :] + back_two[LY - 1 :]
            return carry

        lax.fori_loop(0, LZ, at, 0)
        rows = pl.ds(d * LZ, LZ)
        for side, other in ((0, next_y), (1, last_y)):
            for step in range(2):
                remote(
                    lateral_out.at[side, step, rows],
                    lateral_in.at[side, step, rows],
                    (lateral_s.at[d], lateral_r.at[d]),
                    {"gy": other},
                )

    def layers_send(d):
        wait_bytes(row_in.at[:, pl.ds(0, 2 * LZ)], lateral_r.at[d])

        def add(z, carry):
            at_z = pl.ds(d * LZ + z, 1)
            first, second = lateral_in[0, 0, at_z, :], lateral_in[0, 1, at_z, :]
            third, fourth = lateral_in[1, 0, at_z, :], lateral_in[1, 1, at_z, :]
            moved[d, z, :8] += jnp.where(
                short_row == 0, first, jnp.where(short_row == 1, second, 0.0)
            )
            moved[d, z, LY - 8 :] += jnp.where(
                short_row == 6, third, jnp.where(short_row == 7, fourth, 0.0)
            )
            return carry

        lax.fori_loop(0, LZ, add, 0)
        end = LZ - 1
        layer_out[0, d, 0] = moved[d, end] * weight_z[3, end] + moved[d, end - 1] * weight_z[4, end - 1]
        layer_out[0, d, 1] = moved[d, end] * weight_z[4, end]
        layer_out[1, d, 0] = moved[d, 0] * weight_z[0, 0]
        layer_out[1, d, 1] = moved[d, 0] * weight_z[1, 0] + moved[d, 1] * weight_z[0, 1]
        for side, other in ((0, next_z), (1, last_z)):
            remote(
                layer_out.at[side, d],
                layer_in.at[side, d],
                (layer_s.at[d], layer_r.at[d]),
                {"gz": other},
            )
        for z in range(LZ):
            total = moved[d, z] * weight_z[2, z]
            for offset in (-2, -1, 1, 2):
                if 0 <= z - offset < LZ:
                    total = total + moved[d, z - offset] * weight_z[offset + 2, z - offset]
            result[d, z] = total

    def finish(d):
        wait_bytes(layer_in.at[:, d], layer_r.at[d])
        for side, start in ((0, 0), (1, LZ - 2)):
            for step in range(2):
                result[d, start + step] += layer_in[side, d, step]
        pltpu.make_async_copy(result.at[d], result_out.at[0, d], store_s.at[3 + d]).start()

    velocity_of(0)
    weights(weight_x, 0)
    stretch(0)
    velocity_of(1)
    weights(weight_y, 1)
    lateral_send(0)
    stretch(1)
    velocity_of(2)
    weights(weight_z, 2)
    layers_send(0)
    lateral_send(1)
    stretch(2)
    layers_send(1)
    finish(0)
    lateral_send(2)
    layers_send(2)
    finish(1)
    finish(2)

    for c in range(3):
        wait_bytes(send.at[c, pl.ds(0, (PEERS - 1) * LZ)], ssem.at[c])
        wait_bytes(send.at[c, pl.ds(0, (PEERS - 1) * LZ)], ssem2.at[c])
        wait_bytes(speed.at[c, pl.ds(0, 2)], plane_s.at[c])
        wait_bytes(row_out.at[0, pl.ds(0, 2 * LZ)], row_s.at[c])
        wait_bytes(row_out.at[:, pl.ds(0, 2 * LZ)], lateral_s.at[c])
        wait_bytes(layer_out.at[:, c], layer_s.at[c])
        wait_bytes(result.at[c], store_s.at[c])
        wait_bytes(result.at[c], store_s.at[3 + c])

        @pl.when(grp == 0)
        def _():
            wait_bytes(column_out.at[c], column_s.at[c])
            wait_bytes(ghost_out.at[c], ghost_s.at[c])


def body(vorticity, wind):
    tables = [jnp.asarray(t) for t in make_tables()]
    vmem = pl.BlockSpec(memory_space=pltpu.VMEM)
    shape = jax.ShapeDtypeStruct(vorticity.shape, jnp.float32)
    block = (3, LZ, LY, N)
    buffers = [
        (3, PEERS * LZ, 128),
        (3, GY, N, 128),
        (3, 2, N, N),
        (3, GY, N, 128),
        (3, PEERS * LZ, 128),
        (2, N, N),
        (3, LZ + 2, LY, N),
        (5, LZ, LY, N),
        (5, LZ, LY, N),
        (5, LZ, LY, N),
        block,
        block,
        (2, 3 * LZ, N),
        (2, 3 * LZ, N),
        (3, LY, 128),
        (3, LY, 128),
        (3, LY, 128),
        (3, LY, 128),
        (2, 2, 3 * LZ, N),
        (2, 2, 3 * LZ, N),
        (2, 3, 2, LY, N),
        (2, 3, 2, LY, N),
    ]
    result, velocity = pl.pallas_call(
        step_kernel,
        out_shape=(shape, shape),
        in_specs=[vmem, pl.BlockSpec(memory_space=pltpu.SMEM)] + [vmem] * 5,
        out_specs=(pl.BlockSpec(memory_space=pl.ANY), pl.BlockSpec(memory_space=pl.ANY)),
        scratch_shapes=[pltpu.VMEM(b, jnp.float32) for b in buffers]
        + [pltpu.SemaphoreType.DMA((3,))] * 16
        + [pltpu.SemaphoreType.DMA((6,))],
        compiler_params=pltpu.CompilerParams(collective_id=0, has_side_effects=True),
    )(vorticity, wind, *tables)
    return result, velocity


def solution(mesh):
    return jax.shard_map(
        body,
        mesh=mesh,
        in_specs=(P("grp", None, "gz", "gy", None), P("grp", None)),
        out_specs=(P("grp", None, "gz", "gy", None), P("grp", None, "gz", "gy", None)),
        check_vma=False,
    )
```

time: 162 us -> 117 us (0.72); the launches traced: 162 us -> 114 us
  Pallas kernels: 83 us -> 110 us
  starting transfers between devices: 24.9 us -> 0 us
  other arithmetic: 21.6 us -> 0 us
  waiting for transfers between devices: 18 us -> 0 us
  local copies, waits for them, and re-layouts: 13.1 us -> 3.97 us
    pallas_call x1, Pallas kernels: 83 us -> 110 us  [body(): pl.pallas_call(step_kernel, out_shape=(shape, shape), in_specs=[vmem, pl....]
    ppermute x10 -> x0, starting transfers between devices: 24.9 us -> none  [the longest x2 13.8 us: shifted(): lax.ppermute(value, axis, [(source, source + steps) for source in range(i...]
    ppermute x10 -> x0, waiting for transfers between devices: 18 us -> none  [the longest x2 9.38 us: extended_2(): lax.ppermute(tail, axis, [(i, (i + 1) % count) for i in range(count)])]
    slice x10 -> x0, local copies, waits for them, and re-layouts: 7.62 us -> none  [the longest x2 2.89 us: padded(): initial = lax.slice_in_dim(array, 0, width, axis=dim)]
    select_n x4 -> x0, other arithmetic: 6.72 us -> none  [the longest x1 5.23 us: kernel_weight(): return jnp.where(mag < 1.0, inner, jnp.where(mag < 2.0, outer, 0.0 * mag))]
    add x3 -> x0, other arithmetic: 6.58 us -> none  [the longest x1 3 us: body(): field + TIME_STEP * (field[0:1] * grad_x + field[1:2] * grad_y + field[2:...]
    mul x4 -> x0, other arithmetic: 5.07 us -> none  [the longest x1 1.45 us: body(): rim_rows[:3, :, start:start + width_y, :]]
    broadcast_in_dim x1 -> x0, other arithmetic: 1.94 us -> none  [body(): return (result[None], velocity[None])]
  transfers between devices with their start and end apart: 10 -> 0, of which waited for: 4 -> 0; matrix products, arithmetic and copies ran while one was open for 8% -> 0% of each run, Pallas kernels for 0% -> 0%
where the time goes in v1:
time: 117 us; the launch traced here: 114 us
  Pallas kernels  110 us (94%)
  local copies, waits for them, and re-layouts  3.97 us (3%)
    pallas_call x1, Pallas kernels, body(): pl.pallas_call(step_kernel, out_shape=(shape, shape), in_specs=[vmem, pl....  110 us
    unnamed x4, local copies, waits for them, and re-layouts  3.97 us

profile of v1, /device:TPU:0, one launch (start us, length us, event | category | flops | bytes accessed | tf_op | source)
XLA Modules:
  0.0 114.3 jit_solution(6760197593273667118)
XLA Ops:
  0.6 109.7 %shard_map.86 = (f32[1,3,8,64,256]{4,3,2,1,0:T(8,128)}, f32[1,3,8,64,256]{4,3,2,1,0:T(8,128)}) custom-call(f32[1,3,8,64,256]{4,3,2,1,0:T(8,128)} %field.1, f32[1,3]{1,0:T(1,128)} %wind.1, bf16[2,256,256]{2,1,0:T(8,128)(2,1)} %constant.10.clone.x_in, bf16[2,512,512]{2,1,0:T(8,128)(2,1)} %constant.11.clone.y_in, ...), custom_call_target="tpu_custom_call" | custom-call | tf_op jit(solution)/shard_map/pallas_call | solution.py:477
  110.3 0.0 copy-start
  110.3 2.8 %copy.11 = f32[1,3,8,64,256]{4,3,2,1,0:T(8,128)} copy(f32[1,3,8,64,256]{4,3,2,1,0:T(8,128)} %get-tuple-element.4) | data formatting | bytes 3145728
  113.2 0.0 copy-done
  113.2 1.1 copy.12
Async XLA Ops:
  110.3 2.8 %copy-start = (f32[1,3,8,64,256]{4,3,2,1,0:T(8,128)S(1)}, f32[1,3,8,64,256]{4,3,2,1,0:T(8,128)}, u32[]{:S(2)}) copy-start(f32[1,3,8,64,256]{4,3,2,1,0:T(8,128)} %get-tuple-element.5) | copy-start | bytes 4718596

commit v2 on v1

--- a/solution.py
+++ b/solution.py
@@ -99,12 +99,12 @@
 
 
 def step_kernel(
-    field, wind, x_in, y_in, z_all, y_out, x_out, result_out, velocity_out,
-    send, recv, stream, send2, recv2, scale, speed, weight_x, weight_y, weight_z,
-    moved, result, row_out, row_in, column_out, column_in, ghost_out, ghost_in,
+    field_in, wind, x_in_h, y_in_h, z_all_h, y_out_h, x_out_h, result, speed,
+    field, x_in, y_in, z_all, y_out, x_out, send, recv, stream, send2, recv2, scale, weight_x, weight_y, weight_z,
+    moved, row_out, row_in, column_out, column_in, ghost_out, ghost_in,
     lateral_out, lateral_in, layer_out, layer_in,
     ssem, rsem, ssem2, rsem2, plane_s, plane_r, row_s, row_r, column_s, column_r,
-    ghost_s, ghost_r, lateral_s, lateral_r, layer_s, layer_r, store_s,
+    ghost_s, ghost_r, lateral_s, lateral_r, layer_s, layer_r, load_s,
 ):
     grp = lax.axis_index("grp")
     gy = lax.axis_index("gy")
@@ -125,12 +125,24 @@
             barrier, inc=1, device_id={"gy": other_y, "gz": other_z}, device_id_type=MESH
         )
 
+    def load(source, target, index):
+        pltpu.make_async_copy(source, target, load_s.at[index]).start()
+
+    load(x_in_h, x_in, 3)
+    for c in (1, 2, 0):
+        load(field_in.at[0, c], field.at[0, c], c)
+    load(y_in_h, y_in, 4)
+    load(z_all_h, z_all, 5)
+    load(y_out_h, y_out, 6)
+    load(x_out_h, x_out, 7)
     each_peer(gy, gz, greet)
     pl.semaphore_signal(barrier, inc=1, device_id={"grp": 1 - grp}, device_id_type=MESH)
 
     lane = lax.broadcasted_iota(jnp.int32, (HALF, 128), 1)
     first_half = lane < LY
+    wait_bytes(x_in, load_s.at[3])
     for c in (1, 2, 0):
+        wait_bytes(field.at[0, c], load_s.at[c])
         for b in range(2):
             rows = field[0, c, 4 * b : 4 * b + 4].reshape(4 * LY, N)
             lines = dot3((x_in[0], x_in[1]), split(rows), ((1,), (1,)))
@@ -173,6 +185,10 @@
         scale[0] = 0.5 * (base + top)
         scale[1] = 0.5 * (base - top)
 
+    wait_bytes(y_in, load_s.at[4])
+    wait_bytes(z_all, load_s.at[5])
+    wait_bytes(y_out, load_s.at[6])
+    wait_bytes(x_out, load_s.at[7])
     curl = (curl_x, curl_y, curl_z)
     table_y = (y_in[0], y_in[1])
     cosine = (z_all[0, 0], z_all[1, 0])
@@ -215,6 +231,7 @@
         for j in range(GY):
             send2[d, j] = plane[:, 128 * j : 128 * j + 128]
 
+    def send_back(d):
         def out(other_y, other_z):
             remote(
                 send2.at[d, other_y, pl.ds(pl.multiple_of(other_z * LZ, LZ), LZ)],
@@ -229,8 +246,10 @@
     forward(1)
     forward(2)
     backward(0)
+    send_back(0)
     forward(0)
     backward(1)
+    send_back(1)
     backward(2)
 
     row = lax.broadcasted_iota(jnp.int32, (LY, N), 0)
@@ -270,10 +289,6 @@
         def _():
             remote(column_out.at[d], column_in.at[d], (column_s.at[d], column_r.at[d]), {"grp": 1})
 
-        pltpu.make_async_copy(
-            speed.at[d, pl.ds(1, LZ)], velocity_out.at[0, d], store_s.at[d]
-        ).start()
-
     def weights(target, d):
         def at(z, carry):
             shift = TIME_STEP * speed[d, z + 1]
@@ -408,9 +423,9 @@
         for side, start in ((0, 0), (1, LZ - 2)):
             for step in range(2):
                 result[d, start + step] += layer_in[side, d, step]
-        pltpu.make_async_copy(result.at[d], result_out.at[0, d], store_s.at[3 + d]).start()
 
     velocity_of(0)
+    send_back(2)
     weights(weight_x, 0)
     stretch(0)
     velocity_of(1)
@@ -436,8 +451,6 @@
         wait_bytes(row_out.at[0, pl.ds(0, 2 * LZ)], row_s.at[c])
         wait_bytes(row_out.at[:, pl.ds(0, 2 * LZ)], lateral_s.at[c])
         wait_bytes(layer_out.at[:, c], layer_s.at[c])
-        wait_bytes(result.at[c], store_s.at[c])
-        wait_bytes(result.at[c], store_s.at[3 + c])
 
         @pl.when(grp == 0)
         def _():
@@ -445,9 +458,21 @@
             wait_bytes(ghost_out.at[c], ghost_s.at[c])
 
 
+def output_kernel(result, speed, result_out, velocity_out, sems):
+    copies = [
+        pltpu.make_async_copy(speed.at[:, pl.ds(1, LZ)], velocity_out.at[0], sems.at[0]),
+        pltpu.make_async_copy(result, result_out.at[0], sems.at[1]),
+    ]
+    for copy in copies:
+        copy.start()
+    for copy in copies:
+        copy.wait()
+
+
 def body(vorticity, wind):
     tables = [jnp.asarray(t) for t in make_tables()]
-    vmem = pl.BlockSpec(memory_space=pltpu.VMEM)
+    anywhere = pl.BlockSpec(memory_space=pl.ANY)
+    near = pl.BlockSpec(memory_space=pltpu.VMEM)
     shape = jax.ShapeDtypeStruct(vorticity.shape, jnp.float32)
     block = (3, LZ, LY, N)
     buffers = [
@@ -457,11 +482,9 @@
         (3, GY, N, 128),
         (3, PEERS * LZ, 128),
         (2, N, N),
-        (3, LZ + 2, LY, N),
         (5, LZ, LY, N),
         (5, LZ, LY, N),
         (5, LZ, LY, N),
-        block,
         block,
         (2, 3 * LZ, N),
         (2, 3 * LZ, N),
@@ -474,17 +497,28 @@
         (2, 3, 2, LY, N),
         (2, 3, 2, LY, N),
     ]
-    result, velocity = pl.pallas_call(
+    result, speed = pl.pallas_call(
         step_kernel,
-        out_shape=(shape, shape),
-        in_specs=[vmem, pl.BlockSpec(memory_space=pltpu.SMEM)] + [vmem] * 5,
-        out_specs=(pl.BlockSpec(memory_space=pl.ANY), pl.BlockSpec(memory_space=pl.ANY)),
-        scratch_shapes=[pltpu.VMEM(b, jnp.float32) for b in buffers]
+        out_shape=(pltpu.VMEM(block, jnp.float32), pltpu.VMEM((3, LZ + 2, LY, N), jnp.float32)),
+        in_specs=[anywhere, pl.BlockSpec(memory_space=pltpu.SMEM)] + [anywhere] * 5,
+        out_specs=(pl.BlockSpec(memory_space=pltpu.VMEM), pl.BlockSpec(memory_space=pltpu.VMEM)),
+        scratch_shapes=[pltpu.VMEM(vorticity.shape, jnp.float32)]
+        + [pltpu.VMEM(t.shape, jnp.bfloat16) for t in tables]
+        + [pltpu.VMEM(b, jnp.float32) for b in buffers]
         + [pltpu.SemaphoreType.DMA((3,))] * 16
-        + [pltpu.SemaphoreType.DMA((6,))],
+        + [pltpu.SemaphoreType.DMA((8,))],
         compiler_params=pltpu.CompilerParams(collective_id=0, has_side_effects=True),
     )(vorticity, wind, *tables)
-    return result, velocity
+    return pl.pallas_call(
+        output_kernel,
+        out_shape=(shape, shape),
+        in_specs=[near, near],
+        out_specs=(anywhere, anywhere),
+        scratch_shapes=[pltpu.SemaphoreType.DMA((2,))],
+    )(
+        pltpu.with_memory_space_constraint(result, pltpu.VMEM),
+        pltpu.with_memory_space_constraint(speed, pltpu.VMEM),
+    )
 
 
 def solution(mesh):

time: 117 us -> 105 us (0.90)
  Pallas kernels: 110 us -> 102 us
  local copies, waits for them, and re-layouts: 3.97 us -> 0 us
    pallas_call x1 -> x2, Pallas kernels: 110 us -> 102 us  [the longest x1 101 us: body(): pl.pallas_call(step_kernel, out_shape=(pltpu.VMEM(block, jnp.float32), pl...]
    unnamed x4 -> x0, local copies, waits for them, and re-layouts: 3.97 us -> none
where the time goes in v2:
time: 105 us; the launch traced here: 103 us
  Pallas kernels  102 us (97%)
    pallas_call x1, Pallas kernels, body(): pl.pallas_call(step_kernel, out_shape=(pltpu.VMEM(block, jnp.float32), pl...  101 us

profile of v2, /device:TPU:0, one launch (start us, length us, event | category | flops | bytes accessed | tf_op | source)
XLA Modules:
  0.0 103.1 jit_solution(5683021170108666009)
XLA Ops:
  0.6 100.8 %shard_map.86 = (f32[3,8,64,256]{3,2,1,0:T(8,128)S(1)}, f32[3,10,64,256]{3,2,1,0:T(8,128)S(1)}) custom-call(f32[1,3,8,64,256]{4,3,2,1,0:T(8,128)} %field_in.1, f32[1,3]{1,0:T(1,128)} %wind.1, bf16[2,256,256]{2,1,0:T(8,128)(2,1)} %constant.10.clone.x_in_h, bf16[2,512,512]{2,1,0:T(8,128)(2,1)} %constant.11.clone.y_in_h, ...), custom_call_target="tpu_custom_call" | custom-call | tf_op jit(solution)/shard_map/pallas_call | solution.py:500
  101.4 1.7 %shard_map.87 = (f32[1,3,8,64,256]{4,3,2,1,0:T(8,128)}, f32[1,3,8,64,256]{4,3,2,1,0:T(8,128)}) custom-call(f32[3,8,64,256]{3,2,1,0:T(8,128)S(1)} %get-tuple-element.4.result, f32[3,10,64,256]{3,2,1,0:T(8,128)S(1)} %get-tuple-element.5.speed), custom_call_target="tpu_custom_call" | custom-call | tf_op jit(solution)/shard_map/pallas_call | solution.py:512

commit v3 on v2

--- a/solution.py
+++ b/solution.py
@@ -49,9 +49,11 @@
     to_real = np.concatenate([cos_y, sin_y], 1).reshape(2 * N, N)
     to_imag = np.concatenate([-sin_y, cos_y], 1).reshape(2 * N, N)
     y_in = np.concatenate([to_real, to_imag], 1)
-    y_out = np.concatenate([to_real, to_imag], 1).T / N
     z_all = np.stack([cosine, sine])
-    return [table_pair(t) for t in (x_in, y_in, z_all, y_out, x_out)]
+    edges = x_out[:, [N - 3, N - 2, N - 1, 0]].T.reshape(4, 2, HALF, 1)
+    x_edge = np.broadcast_to(edges, (4, 2, HALF, LY)).transpose(0, 2, 1, 3).reshape(4, HALF, 128)
+    pairs = [table_pair(t) for t in (x_in, y_in, z_all, x_out)]
+    return pairs + [np.asarray(x_edge, np.float32)]
 
 
 def dot3(a, b, dims=((1,), (0,))):
@@ -99,12 +101,14 @@
 
 
 def step_kernel(
-    field_in, wind, x_in_h, y_in_h, z_all_h, y_out_h, x_out_h, result, speed,
-    field, x_in, y_in, z_all, y_out, x_out, send, recv, stream, send2, recv2, scale, weight_x, weight_y, weight_z,
-    moved, row_out, row_in, column_out, column_in, ghost_out, ghost_in,
+    field_in, wind, x_in_h, y_in_h, z_all_h, x_out_h, x_edge_h, result, speed,
+    field, x_in, y_in, z_all, x_out, x_edge, send, recv, stream, send2, recv2, scale, weight_x, weight_y, weight_z,
+    moved, row_out, row_in, edge_out, edge_in, field_edge_out, field_edge_in,
     lateral_out, lateral_in, layer_out, layer_in,
-    ssem, rsem, ssem2, rsem2, plane_s, plane_r, row_s, row_r, column_s, column_r,
-    ghost_s, ghost_r, lateral_s, lateral_r, layer_s, layer_r, load_s,
+    near_out, near_in, corner_in, corner,
+    ssem, rsem, ssem2, rsem2, plane_s, plane_r, row_s, row_r, edge_s, edge_r,
+    lateral_s, lateral_r, layer_s, layer_r, load_s,
+    near_s, near_r, corner_s, corner_r,
 ):
     grp = lax.axis_index("grp")
     gy = lax.axis_index("gy")
@@ -133,10 +137,14 @@
         load(field_in.at[0, c], field.at[0, c], c)
     load(y_in_h, y_in, 4)
     load(z_all_h, z_all, 5)
-    load(y_out_h, y_out, 6)
-    load(x_out_h, x_out, 7)
+    load(x_out_h, x_out, 6)
+    load(x_edge_h, x_edge, 7)
     each_peer(gy, gz, greet)
-    pl.semaphore_signal(barrier, inc=1, device_id={"grp": 1 - grp}, device_id_type=MESH)
+    around = ({}, {"gy": next_y}, {"gy": last_y}, {"gz": next_z}, {"gz": last_z})
+    for place in around:
+        pl.semaphore_signal(
+            barrier, inc=1, device_id={"grp": 1 - grp, **place}, device_id_type=MESH
+        )
 
     lane = lax.broadcasted_iota(jnp.int32, (HALF, 128), 1)
     first_half = lane < LY
@@ -156,7 +164,18 @@
                 send[c, pl.ds(z + 1, HALF, stride=LZ), :] = odd
     mine = pl.ds(pl.multiple_of(me * LZ, LZ), LZ)
     mine_z = pl.ds(pl.multiple_of(gz * LZ, LZ), LZ)
-    pl.semaphore_wait(barrier, PEERS)
+
+    @pl.when(grp == 0)
+    def _():
+        for c in range(3):
+            for z in range(0, LZ, 2):
+                turned = field[0, c, z : z + 2, :, 128:].reshape(2 * LY, 128).T[120:]
+                other = pltpu.roll(turned, LY, 1)
+                for q in range(2):
+                    field_edge_out[c, q, z : z + 1, :] = turned[6 + q : 7 + q]
+                    field_edge_out[c, q, z + 1 : z + 2, :] = other[6 + q : 7 + q]
+
+    pl.semaphore_wait(barrier, PEERS - 1 + len(around))
 
     for c in (1, 2, 0):
         def out(other_y, other_z, c=c):
@@ -171,6 +190,10 @@
         each_peer(gy, gz, out)
         recv[c, gy, mine_z, :] = send[c, mine, :]
 
+    @pl.when(grp == 0)
+    def _():
+        remote(field_edge_out, field_edge_in, (load_s.at[8], load_s.at[9]), {"grp": 1})
+
     wave_z, curl_z = waves((N, N), 0)
     wave_y, curl_y = waves((N, N), 1)
     curl_x = me.astype(jnp.float32) * (2.0 * math.pi / N)
@@ -187,8 +210,8 @@
 
     wait_bytes(y_in, load_s.at[4])
     wait_bytes(z_all, load_s.at[5])
-    wait_bytes(y_out, load_s.at[6])
-    wait_bytes(x_out, load_s.at[7])
+    wait_bytes(x_out, load_s.at[6])
+    wait_bytes(x_edge, load_s.at[7])
     curl = (curl_x, curl_y, curl_z)
     table_y = (y_in[0], y_in[1])
     cosine = (z_all[0, 0], z_all[1, 0])
@@ -226,8 +249,8 @@
         by_sin = dot3(sine, lines)
         real = by_cos[:, :N] - by_sin[:, N:]
         imag = by_cos[:, N:] + by_sin[:, :N]
-        lines = split(jnp.concatenate([real, imag], 1) * (1.0 / N))
-        plane = dot3(lines, (y_out[0], y_out[1]))
+        lines = split(jnp.concatenate([real, imag], 1) * (1.0 / (N * N)))
+        plane = dot3(lines, table_y, ((1,), (1,)))
         for j in range(GY):
             send2[d, j] = plane[:, 128 * j : 128 * j + 128]
 
@@ -259,12 +282,14 @@
     no_wrap_low = jnp.where(is_wake, 0, -N)
     no_wrap_high = jnp.where(is_wake, N, 2 * N)
     first_column = jnp.where(is_wake, 0, -1)
+    small_lane = lax.broadcasted_iota(jnp.int32, (LZ, 128), 1)
+    small_row = lax.broadcasted_iota(jnp.int32, (LZ, 128), 0)
     last_column = jnp.where(is_wake, N - 1, N)
 
     def velocity_of(d):
         wait_bytes(recv.at[0, :, pl.ds(0, (PEERS - 1) * LZ // GY)], rsem2.at[d])
         drift = wind[0, d]
-        edge = jnp.zeros((LY, 128), jnp.float32)
+
         for b in range(2):
             parts = []
             for z in range(4 * b, 4 * b + 4):
@@ -277,17 +302,47 @@
                 speed[d, z + 1] = plane
                 row_out[0, d * LZ + z : d * LZ + z + 1, :] = plane[LY - 1 :]
                 row_out[1, d * LZ + z : d * LZ + z + 1, :] = plane[:1]
-                edge = jnp.where(tile == z, pltpu.roll(plane[:, 128:], z + 1, 1), edge)
-        column_out[d] = edge
+                if d == 2 and z in (0, 1, LZ - 2, LZ - 1):
+                    side, start = (1, 4 * z) if z < 2 else (0, 4 * (z - LZ + 2))
+                    near_out[side, start : start + 2, :] = plane[:2]
+                    near_out[side, start + 2 : start + 4, :] = plane[LY - 2 :]
+            if b == 0:
+                remote(
+                    speed.at[d, 1],
+                    speed.at[d, LZ + 1],
+                    (plane_s.at[d], plane_r.at[d]),
+                    {"gz": last_z},
+                )
         rows = pl.ds(d * LZ, LZ)
         remote(speed.at[d, LZ], speed.at[d, 0], (plane_s.at[d], plane_r.at[d]), {"gz": next_z})
-        remote(speed.at[d, 1], speed.at[d, LZ + 1], (plane_s.at[d], plane_r.at[d]), {"gz": last_z})
         remote(row_out.at[0, rows], row_in.at[0, rows], (row_s.at[d], row_r.at[d]), {"gy": next_y})
         remote(row_out.at[1, rows], row_in.at[1, rows], (row_s.at[d], row_r.at[d]), {"gy": last_y})
+        if d == 2:
+            for side, other in ((0, next_z), (1, last_z)):
+                remote(near_out.at[side], near_in.at[side], (near_s, near_r), {"gz": other})
 
         @pl.when(grp == 0)
         def _():
-            remote(column_out.at[d], column_in.at[d], (column_s.at[d], column_r.at[d]), {"grp": 1})
+            def add(i, totals):
+                for k in range(8):
+                    line = 8 * i + k
+                    lines = recv2[d, pl.ds(pl.multiple_of(line * LZ, LZ), LZ), :]
+                    totals = [t + lines * x_edge[q, pl.ds(line, 1), :] for q, t in enumerate(totals)]
+                return tuple(totals)
+
+            zero = jnp.zeros((LZ, 128), jnp.float32)
+            totals = lax.fori_loop(0, HALF // 8, add, (zero,) * 4)
+            for q in range(4):
+                edge_out[d, q] = totals[q] + pltpu.roll(totals[q], LY, 1) + drift
+            sems = (edge_s.at[d], edge_r.at[d])
+            remote(edge_out.at[d], edge_in.at[d, 0], sems, {"grp": 1})
+            for slot in range(1, 5):
+                remote(
+                    edge_out.at[d, pl.ds(1, 2)],
+                    edge_in.at[d, slot, pl.ds(1, 2)],
+                    sems,
+                    {"grp": 1, **around[slot]},
+                )
 
     def weights(target, d):
         def at(z, carry):
@@ -307,21 +362,16 @@
         wait_bytes(speed.at[d, pl.ds(0, 2)], plane_r.at[d])
         wait_bytes(row_in.at[0, pl.ds(0, 2 * LZ)], row_r.at[d])
 
-        @pl.when(is_wake)
-        def _():
-            wait_bytes(column_in.at[d], column_r.at[d])
-
-        def at(z, ghost):
+        def at(z, carry):
             here = speed[d, z + 1]
             grad_z = speed[d, z + 2] - speed[d, z]
             low = row_in[0, pl.ds(d * LZ + z, 1), :]
             high = row_in[1, pl.ds(d * LZ + z, 1), :]
             up = jnp.where(row == LY - 1, high, moved_by(here, -1, 0))
             down = jnp.where(row == 0, low, moved_by(here, 1, 0))
-            inflow = pltpu.roll(column_in[d], lax.rem(128 - z, 128), 1)
             left = moved_by(here, 1, 1)
             left = jnp.concatenate(
-                [jnp.where(tile == first_column, inflow, left[:, :128]), left[:, 128:]], 1
+                [jnp.where(tile == first_column, 0.0, left[:, :128]), left[:, 128:]], 1
             )
             right = jnp.where(column == last_column, here, moved_by(here, -1, 1))
             strength = field[0, d, z] + (0.5 * TIME_STEP) * (
@@ -334,23 +384,51 @@
             total = strength * weight_x[2, z] + one + two
             total = total + moved_by(strength * weight_x[1, z], -1, 1)
             moved[d, z] = total + moved_by(strength * weight_x[0, z], -2, 1)
-            over = jnp.where(tile == 0, one[:, :128], 0.0) + jnp.where(tile < 2, two[:, :128], 0.0)
-            return ghost + pltpu.roll(over, 2 * z, 1)
-
-        ghost_out[d] = lax.fori_loop(0, LZ, at, jnp.zeros((LY, 128), jnp.float32))
-
-        @pl.when(grp == 0)
-        def _():
-            remote(ghost_out.at[d], ghost_in.at[d], (ghost_s.at[d], ghost_r.at[d]), {"grp": 1})
+            return carry
+
+        lax.fori_loop(0, LZ, at, 0)
 
     def lateral_send(d):
         @pl.when(is_wake)
         def _():
-            wait_bytes(ghost_in.at[d], ghost_r.at[d])
+            wait_bytes(edge_in.at[d, pl.ds(0, 3)], edge_r.at[d])
+            if d == 0:
+                wait_bytes(field_edge_in, load_s.at[9])
+
+            def particle(q, grad_x):
+                here = edge_in[d, 0, q]
+                low_y, high_y = edge_in[d, 1, q], edge_in[d, 2, q]
+                low_z, high_z = edge_in[d, 3, q], edge_in[d, 4, q]
+                up = jnp.where(small_lane == LY - 1, moved_by(high_y, -1, 1), moved_by(here, -1, 1))
+                down = jnp.where(small_lane == 0, moved_by(low_y, 1, 1), moved_by(here, 1, 1))
+                above = jnp.where(small_row == LZ - 1, moved_by(high_z, -1, 0), moved_by(here, -1, 0))
+                below = jnp.where(small_row == 0, moved_by(low_z, 1, 0), moved_by(here, 1, 0))
+                return field_edge_in[d, q - 1] + (0.5 * TIME_STEP) * (
+                    field_edge_in[0, q - 1] * grad_x
+                    + field_edge_in[1, q - 1] * (up - down)
+                    + field_edge_in[2, q - 1] * (above - below)
+                )
+
+            strength_one = particle(2, edge_in[d, 0, 3] - edge_in[d, 0, 1])
+            strength_two = particle(1, edge_in[d, 0, 2] - edge_in[d, 0, 0])
+            shift_one = TIME_STEP * edge_in[0, 0, 2]
+            shift_two = TIME_STEP * edge_in[0, 0, 1]
+            first = strength_one * kernel_weight(1 - shift_one) + strength_two * kernel_weight(
+                2 - shift_two
+            )
+            second = strength_one * kernel_weight(2 - shift_one)
+            empty = jnp.zeros((128 - 3 * LZ, 128), jnp.float32)
+            turned = jnp.concatenate([edge_in[d, 0, 2], first, second, empty], 0).T[:LY]
 
             def add(z, carry):
-                inflow = pltpu.roll(ghost_in[d], lax.rem(128 - 2 * z, 128), 1)
-                moved[d, z, :, :128] += jnp.where(tile < 2, inflow, 0.0)
+                inflow = jnp.where(tile == 0, pltpu.roll(turned, lax.rem(128 - z, 128), 1), 0.0)
+                missing = (-0.5 * TIME_STEP) * field[0, 0, z, :, :128] * inflow
+                total = missing * weight_x[2, z, :, :128]
+                total = total + pltpu.roll(missing * weight_x[3, z, :, :128], 1, 1)
+                total = total + pltpu.roll(missing * weight_x[4, z, :, :128], 2, 1)
+                total = total + jnp.where(tile == 0, pltpu.roll(turned, 120 - z, 1), 0.0)
+                total = total + jnp.where(tile == 1, pltpu.roll(turned, 113 - z, 1), 0.0)
+                moved[d, z, :, :128] += total
                 return carry
 
             lax.fori_loop(0, LZ, add, 0)
@@ -382,23 +460,36 @@
                     (lateral_s.at[d], lateral_r.at[d]),
                     {"gy": other},
                 )
+        if d == 2:
+            for side, other in ((0, next_y), (1, last_y)):
+                for level, far in ((0, next_z), (1, last_z)):
+                    remote(
+                        lateral_out.at[side, :, rows],
+                        corner_in.at[side, level],
+                        (corner_s, corner_r),
+                        {"gy": other, "gz": far},
+                    )
+
+    def lateral_rows(d, z):
+        at_z = pl.ds(d * LZ + z, 1)
+        first, second = lateral_in[0, 0, at_z, :], lateral_in[0, 1, at_z, :]
+        third, fourth = lateral_in[1, 0, at_z, :], lateral_in[1, 1, at_z, :]
+        low = jnp.where(short_row == 0, first, jnp.where(short_row == 1, second, 0.0))
+        high = jnp.where(short_row == 6, third, jnp.where(short_row == 7, fourth, 0.0))
+        return low, high
+
+    def lateral_add(d):
+        wait_bytes(row_in.at[:, pl.ds(0, 2 * LZ)], lateral_r.at[d])
+
+        def add(z, carry):
+            low, high = lateral_rows(d, z)
+            moved[d, z, :8] += low
+            moved[d, z, LY - 8 :] += high
+            return carry
+
+        lax.fori_loop(0, LZ, add, 0)
 
     def layers_send(d):
-        wait_bytes(row_in.at[:, pl.ds(0, 2 * LZ)], lateral_r.at[d])
-
-        def add(z, carry):
-            at_z = pl.ds(d * LZ + z, 1)
-            first, second = lateral_in[0, 0, at_z, :], lateral_in[0, 1, at_z, :]
-            third, fourth = lateral_in[1, 0, at_z, :], lateral_in[1, 1, at_z, :]
-            moved[d, z, :8] += jnp.where(
-                short_row == 0, first, jnp.where(short_row == 1, second, 0.0)
-            )
-            moved[d, z, LY - 8 :] += jnp.where(
-                short_row == 6, third, jnp.where(short_row == 7, fourth, 0.0)
-            )
-            return carry
-
-        lax.fori_loop(0, LZ, add, 0)
         end = LZ - 1
         layer_out[0, d, 0] = moved[d, end] * weight_z[3, end] + moved[d, end - 1] * weight_z[4, end - 1]
         layer_out[0, d, 1] = moved[d, end] * weight_z[4, end]
@@ -418,6 +509,35 @@
                     total = total + moved[d, z - offset] * weight_z[offset + 2, z - offset]
             result[d, z] = total
 
+    def late_rows(d):
+        wait_bytes(row_in.at[:, pl.ds(0, 2 * LZ)], lateral_r.at[d])
+        for z in range(LZ):
+            for start, part in zip((0, LY - 8), lateral_rows(d, z)):
+                rows = slice(start, start + 8)
+                for offset in range(-2, 3):
+                    if 0 <= z + offset < LZ:
+                        result[d, z + offset, rows] += part * weight_z[offset + 2, z, rows]
+        wait_bytes(near_in, near_r)
+        wait_bytes(corner_in, corner_r)
+        for level in range(2):
+            for plane in range(2):
+                z = plane if level else LZ - 2 + plane
+                for side in range(2):
+                    for step in range(2):
+                        at_row = 4 * plane + 2 * side + step
+                        corner[level, at_row : at_row + 1, :] = corner_in[side, level, step, z : z + 1]
+        shift = TIME_STEP * near_in[0]
+        one = corner[0] * kernel_weight(1 - shift)
+        two = corner[0] * kernel_weight(2 - shift)
+        parts = [(0, one[4:] + two[:4]), (1, two[4:])]
+        shift = TIME_STEP * near_in[1]
+        one = corner[1] * kernel_weight(-1 - shift)
+        two = corner[1] * kernel_weight(-2 - shift)
+        parts += [(LZ - 1, one[:4] + two[4:]), (LZ - 2, two[:4])]
+        for z, part in parts:
+            result[d, z, :2] += part[:2]
+            result[d, z, LY - 2 :] += part[2:]
+
     def finish(d):
         wait_bytes(layer_in.at[:, d], layer_r.at[d])
         for side, start in ((0, 0), (1, LZ - 2)):
@@ -434,16 +554,21 @@
     stretch(1)
     velocity_of(2)
     weights(weight_z, 2)
+    lateral_add(0)
     layers_send(0)
     lateral_send(1)
     stretch(2)
+    lateral_add(1)
     layers_send(1)
-    finish(0)
     lateral_send(2)
     layers_send(2)
+    finish(0)
     finish(1)
+    late_rows(2)
     finish(2)
 
+    wait_bytes(near_out, near_s)
+    wait_bytes(corner_in, corner_s)
     for c in range(3):
         wait_bytes(send.at[c, pl.ds(0, (PEERS - 1) * LZ)], ssem.at[c])
         wait_bytes(send.at[c, pl.ds(0, (PEERS - 1) * LZ)], ssem2.at[c])
@@ -454,8 +579,9 @@
 
         @pl.when(grp == 0)
         def _():
-            wait_bytes(column_out.at[c], column_s.at[c])
-            wait_bytes(ghost_out.at[c], ghost_s.at[c])
+            wait_bytes(edge_in.at[c, pl.ds(0, 3)], edge_s.at[c])
+            if c == 0:
+                wait_bytes(field_edge_out, load_s.at[8])
 
 
 def output_kernel(result, speed, result_out, velocity_out, sems):
@@ -488,14 +614,18 @@
         block,
         (2, 3 * LZ, N),
         (2, 3 * LZ, N),
-        (3, LY, 128),
-        (3, LY, 128),
-        (3, LY, 128),
-        (3, LY, 128),
+        (3, 4, LZ, 128),
+        (3, 5, 4, LZ, 128),
+        (3, 2, LZ, 128),
+        (3, 2, LZ, 128),
         (2, 2, 3 * LZ, N),
         (2, 2, 3 * LZ, N),
         (2, 3, 2, LY, N),
         (2, 3, 2, LY, N),
+        (2, 8, N),
+        (2, 8, N),
+        (2, 2, 2, LZ, N),
+        (2, 8, N),
     ]
     result, speed = pl.pallas_call(
         step_kernel,
@@ -503,10 +633,11 @@
         in_specs=[anywhere, pl.BlockSpec(memory_space=pltpu.SMEM)] + [anywhere] * 5,
         out_specs=(pl.BlockSpec(memory_space=pltpu.VMEM), pl.BlockSpec(memory_space=pltpu.VMEM)),
         scratch_shapes=[pltpu.VMEM(vorticity.shape, jnp.float32)]
-        + [pltpu.VMEM(t.shape, jnp.bfloat16) for t in tables]
+        + [pltpu.VMEM(t.shape, t.dtype) for t in tables]
         + [pltpu.VMEM(b, jnp.float32) for b in buffers]
-        + [pltpu.SemaphoreType.DMA((3,))] * 16
-        + [pltpu.SemaphoreType.DMA((8,))],
+        + [pltpu.SemaphoreType.DMA((3,))] * 14
+        + [pltpu.SemaphoreType.DMA((10,))]
+        + [pltpu.SemaphoreType.DMA] * 4,
         compiler_params=pltpu.CompilerParams(collective_id=0, has_side_effects=True),
     )(vorticity, wind, *tables)
     return pl.pallas_call(

time: 105 us -> 103 us (0.981)
  Pallas kernels: 102 us -> 100 us
    pallas_call x1, Pallas kernels: 101 us -> 98.3 us  [body(): pl.pallas_call(step_kernel, out_shape=(pltpu.VMEM(block, jnp.float32), pl...]
where the time goes in v3:
time: 103 us; the launch traced here: 101 us
  Pallas kernels  100 us (97%)
    pallas_call x1, Pallas kernels, body(): pl.pallas_call(step_kernel, out_shape=(pltpu.VMEM(block, jnp.float32), pl...  98.3 us

profile of v3, /device:TPU:0, one launch (start us, length us, event | category | flops | bytes accessed | tf_op | source)
XLA Modules:
  0.0 100.8 jit_solution(8518370629651570837)
XLA Ops:
  0.6 98.3 %shard_map.86 = (f32[3,8,64,256]{3,2,1,0:T(8,128)S(1)}, f32[3,10,64,256]{3,2,1,0:T(8,128)S(1)}) custom-call(f32[1,3,8,64,256]{4,3,2,1,0:T(8,128)} %field_in.1, f32[1,3]{1,0:T(1,128)} %wind.1, bf16[2,256,256]{2,1,0:T(8,128)(2,1)} %constant.10.clone.x_in_h, bf16[2,512,512]{2,1,0:T(8,128)(2,1)} %constant.11.clone.y_in_h, ...), custom_call_target="tpu_custom_call" | custom-call | tf_op jit(solution)/shard_map/pallas_call | solution.py:630
  99.0 1.7 %shard_map.87 = (f32[1,3,8,64,256]{4,3,2,1,0:T(8,128)}, f32[1,3,8,64,256]{4,3,2,1,0:T(8,128)}) custom-call(f32[3,8,64,256]{3,2,1,0:T(8,128)S(1)} %get-tuple-element.4.result, f32[3,10,64,256]{3,2,1,0:T(8,128)S(1)} %get-tuple-element.5.speed), custom_call_target="tpu_custom_call" | custom-call | tf_op jit(solution)/shard_map/pallas_call | solution.py:643

commit v4 on v3

--- a/solution.py
+++ b/solution.py
@@ -89,11 +89,11 @@
 
 def kernel_weight(offset):
     mag = jnp.abs(offset)
-    square = mag * mag
-    inner = 1.0 + square * (1.5 * mag - 2.5)
-    rest = 2.0 - mag
-    outer = 0.5 * rest * rest * (1.0 - mag)
-    return jnp.where(mag < 1.0, inner, jnp.where(mag < 2.0, outer, 0.0 * mag))
+    inner = 1.0 + mag * mag * (1.5 * mag - 2.5)
+    near = jnp.minimum(mag, 2.0)
+    rest = 2.0 - near
+    outer = rest * rest * (0.5 - 0.5 * near)
+    return jnp.where(mag < 1.0, inner, outer)
 
 
 def moved_by(values, steps, axis):
@@ -502,6 +502,7 @@
                 (layer_s.at[d], layer_r.at[d]),
                 {"gz": other},
             )
+    def layers_within(d):
         for z in range(LZ):
             total = moved[d, z] * weight_z[2, z]
             for offset in (-2, -1, 1, 2):
@@ -562,6 +563,9 @@
     layers_send(1)
     lateral_send(2)
     layers_send(2)
+    layers_within(0)
+    layers_within(1)
+    layers_within(2)
     finish(0)
     finish(1)
     late_rows(2)

time: 103 us -> 102 us (level)
  no operation moved by 1% of the time
where the time goes in v4:
time: 102 us; the launch traced here: 101 us
  Pallas kernels  100 us (98%)
    pallas_call x1, Pallas kernels, body(): pl.pallas_call(step_kernel, out_shape=(pltpu.VMEM(block, jnp.float32), pl...  98.4 us

profile of v4, /device:TPU:0, one launch (start us, length us, event | category | flops | bytes accessed | tf_op | source)
XLA Modules:
  0.0 100.7 jit_solution(6410011602938769537)
XLA Ops:
  0.6 98.4 %shard_map.86 = (f32[3,8,64,256]{3,2,1,0:T(8,128)S(1)}, f32[3,10,64,256]{3,2,1,0:T(8,128)S(1)}) custom-call(f32[1,3,8,64,256]{4,3,2,1,0:T(8,128)} %field_in.1, f32[1,3]{1,0:T(1,128)} %wind.1, bf16[2,256,256]{2,1,0:T(8,128)(2,1)} %constant.10.clone.x_in_h, bf16[2,512,512]{2,1,0:T(8,128)(2,1)} %constant.11.clone.y_in_h, ...), custom_call_target="tpu_custom_call" | custom-call | tf_op jit(solution)/shard_map/pallas_call | solution.py:634
  99.0 1.7 %shard_map.87 = (f32[1,3,8,64,256]{4,3,2,1,0:T(8,128)}, f32[1,3,8,64,256]{4,3,2,1,0:T(8,128)}) custom-call(f32[3,8,64,256]{3,2,1,0:T(8,128)S(1)} %get-tuple-element.4.result, f32[3,10,64,256]{3,2,1,0:T(8,128)S(1)} %get-tuple-element.5.speed), custom_call_target="tpu_custom_call" | custom-call | tf_op jit(solution)/shard_map/pallas_call | solution.py:647

commit v5 on v4

--- a/solution.py
+++ b/solution.py
@@ -589,10 +589,12 @@
 
 
 def output_kernel(result, speed, result_out, velocity_out, sems):
-    copies = [
-        pltpu.make_async_copy(speed.at[:, pl.ds(1, LZ)], velocity_out.at[0], sems.at[0]),
-        pltpu.make_async_copy(result, result_out.at[0], sems.at[1]),
-    ]
+    copies = []
+    for d in range(3):
+        copies += [
+            pltpu.make_async_copy(speed.at[d, pl.ds(1, LZ)], velocity_out.at[0, d], sems.at[d]),
+            pltpu.make_async_copy(result.at[d], result_out.at[0, d], sems.at[3 + d]),
+        ]
     for copy in copies:
         copy.start()
     for copy in copies:
@@ -649,7 +651,7 @@
         out_shape=(shape, shape),
         in_specs=[near, near],
         out_specs=(anywhere, anywhere),
-        scratch_shapes=[pltpu.SemaphoreType.DMA((2,))],
+        scratch_shapes=[pltpu.SemaphoreType.DMA((6,))],
     )(
         pltpu.with_memory_space_constraint(result, pltpu.VMEM),
         pltpu.with_memory_space_constraint(speed, pltpu.VMEM),

time: 102 us -> 102 us (level)
  no operation moved by 1% of the time
where the time goes in v5:
time: 102 us; the launch traced here: 101 us
  Pallas kernels  100 us (98%)
    pallas_call x1, Pallas kernels, body(): pl.pallas_call(step_kernel, out_shape=(pltpu.VMEM(block, jnp.float32), pl...  98.3 us

profile of v5, /device:TPU:0, one launch (start us, length us, event | category | flops | bytes accessed | tf_op | source)
XLA Modules:
  0.0 100.9 jit_solution(14868712499787178052)
XLA Ops:
  0.6 98.3 %shard_map.86 = (f32[3,8,64,256]{3,2,1,0:T(8,128)S(1)}, f32[3,10,64,256]{3,2,1,0:T(8,128)S(1)}) custom-call(f32[1,3,8,64,256]{4,3,2,1,0:T(8,128)} %field_in.1, f32[1,3]{1,0:T(1,128)} %wind.1, bf16[2,256,256]{2,1,0:T(8,128)(2,1)} %constant.10.clone.x_in_h, bf16[2,512,512]{2,1,0:T(8,128)(2,1)} %constant.11.clone.y_in_h, ...), custom_call_target="tpu_custom_call" | custom-call | tf_op jit(solution)/shard_map/pallas_call | solution.py:636
  99.0 1.7 %shard_map.87 = (f32[1,3,8,64,256]{4,3,2,1,0:T(8,128)}, f32[1,3,8,64,256]{4,3,2,1,0:T(8,128)}) custom-call(f32[3,8,64,256]{3,2,1,0:T(8,128)S(1)} %get-tuple-element.4.result, f32[3,10,64,256]{3,2,1,0:T(8,128)S(1)} %get-tuple-element.5.speed), custom_call_target="tpu_custom_call" | custom-call | tf_op jit(solution)/shard_map/pallas_call | solution.py:649
